TPU v7x, 32 devices: a whole 2x2x4 slice. The times are simulated.
32 devices in a mesh: m: 2 (over x), kk: 4 (over z), g: 4 (over y, core).
Axes of the slice: x: 2, y: 2, z: 4, core: 2. Of those that a mesh axis runs over, the one named last changes fastest.
Arguments:
- a_mat: bfloat16 [6144, 8192], P(('m', 'g'), 'kk'), parts along dimension 0
Outputs:
- output: float32 [8, 3, 768, 768], P(('m', 'g'), None, 'kk'), parts along dimension 0
There are 2 independent parts. A program takes and returns all parts, laid end to end along the dimension named above; each array names one.
All inputs are finite; a program needn't handle non-finite values.
Results may differ from a plain program's by a relative error of at most 0.001.
Values are sent between devices in bfloat16 or wider.
A program may use at most 1 GiB of HBM per device.

v0:
```python
import math
import jax
import jax.numpy as jnp
from jax import lax
from jax.sharding import PartitionSpec as P


def block_offsets(groups):
    half_size = groups // 2
    step_width = max(1, math.isqrt(half_size))
    big_count = -(-half_size // step_width)
    small_offs = [step_width - 1 - pos_idx for pos_idx in range(step_width)]
    big_offs = [(pos_idx + 1) * step_width for pos_idx in range(big_count)]
    return half_size, small_offs, big_offs


def solution(mesh):
    groups = mesh.shape["g"]
    half_size, small_offs, big_offs = block_offsets(groups)
    has_empty = 2 * half_size == groups

    def fetch_block(a_blk, offset):
        if offset == 0:
            return a_blk
        perm_pairs = [((dest_pos + offset) % groups, dest_pos) for dest_pos in range(groups)]
        return lax.ppermute(a_blk, "g", perm_pairs)

    def local_fn(a_blk):
        dev_pos = lax.axis_index("g")
        rows_blk = a_blk.shape[0]
        small_stack = jnp.stack([fetch_block(a_blk, offset) for offset in small_offs])
        big_stack = jnp.stack([fetch_block(a_blk, offset) for offset in big_offs])
        diag_blk = lax.dot_general(a_blk, a_blk, (((1,), (1,)), ((), ())), preferred_element_type=jnp.float32)
        cross_blk = jnp.einsum("jrk,isk->jirs", big_stack, small_stack, preferred_element_type=jnp.float32)
        cross_blk = cross_blk.reshape(-1, rows_blk, rows_blk)[:half_size]
        result = jnp.concatenate([diag_blk[None], cross_blk], axis=0)
        if has_empty:
            slot_ids = jnp.arange(half_size + 1)[:, None, None]
            result = jnp.where((slot_ids == half_size) & (dev_pos >= half_size), 0.0, result)
        result = lax.psum_scatter(result, "kk", scatter_dimension=1, tiled=True)
        return result[None]

    return jax.shard_map(local_fn, mesh=mesh, in_specs=(P(("m", "g"), "kk"),), out_specs=P(("m", "g"), None, "kk", None), check_vma=False)
```

profile of v0, /device:TPU:21, one launch (start us, length us, event | category | flops | bytes accessed | tf_op | source)
XLA Modules:
  0.0 252.6 jit_solution(11047605841270944769)
XLA Ops:
  6.5 0.0 reduce-scatter.2.cloned.1.call-start
  6.5 0.7 collective-permute-start
  7.2 0.2 collective-permute-start.1
  7.4 0.0 copy-start
  7.4 5.6 %convolution_bitcast_fusion = f32[1,768,768]{2,1,0:T(8,128)S(1)} fusion(bf16[768,2048]{1,0:T(8,128)(2,1)} %param.1), kind=kOutput, calls=%fused_computation.6 | convolution fusion | flops 2415919104 | bytes 5505024 | tf_op jit(solution)/shard_map/dot_general | solution.py:33
  13.1 63.8 %collective-permute-done = bf16[768,2048]{1,0:T(8,128)(2,1)S(1)} collective-permute-done((bf16[768,2048]{1,0:T(8,128)(2,1)}, bf16[768,2048]{1,0:T(8,128)(2,1)S(1)}, u32[]{:S(2)}, u32[]{:S(2)}) %collective-permute-start) | collective-permute-done | bytes 3145760 | tf_op jit(solution)/shard_map/ppermute | solution.py:26
  76.8 0.6 collective-permute-done.1
  77.4 0.0 copy-done
  77.4 7.1 %fusion = f32[2,768,768]{2,1,0:T(8,128)S(1)} fusion(bf16[1,768,2048]{2,1,0:T(8,128)(2,1)} %bitcast.2, bf16[1,768,2048]{2,1,0:T(8,128)(2,1)S(1)} %bitcast.10, bf16[768,2048]{1,0:T(8,128)(2,1)S(1)} %copy-done), kind=kOutput, calls=%fused_computation.1 | convolution fusion | flops 4834983936 | bytes 14155776 | tf_op jit(solution)/shard_map/jrk,isk->jirs/dot_general | solution.py:34
  84.6 3.5 %maximum_select_fusion = f32[3,768,768]{2,1,0:T(8,128)} fusion(f32[2,768,768]{2,1,0:T(8,128)S(1)} %fusion, f32[1,768,768]{2,1,0:T(8,128)S(1)} %convolution_bitcast_fusion, pred[3]{0:T(512)(128)(4,1)S(1)} %compare_and_fusion), kind=kLoop, calls=%fused_computation | loop fusion | flops 3538944 | bytes 14155779 | tf_op jit(solution)/shard_map/jit(_where)/select_n | solution.py:39
  88.1 0.0 reduce-scatter.2.cloned.1.call-update
  88.2 157.6 %reduce-scatter.2.cloned.1.call-done = f32[3,192,768]{2,1,0:T(8,128)} async-done(((f32[3,768,768]{2,1,0:T(8,128)}), f32[3,192,768]{2,1,0:T(8,128)}) %reduce-scatter.2.cloned.1.call-update) | async-done | bytes 1769488 | tf_op jit(solution)/shard_map/reduce_scatter | solution.py:40
  (1 shorter events, 0.0 us)
Async XLA Ops:
  6.5 239.3 %reduce-scatter.2.cloned.1.call-start = ((), (), s32[]{:S(2)}) async-start(), calls=%async_computation.1 | async-start | bytes 8847360 | tf_op jit(solution)/shard_map/reduce_scatter | solution.py:40
  6.5 70.3 %collective-permute-start = (bf16[768,2048]{1,0:T(8,128)(2,1)}, bf16[768,2048]{1,0:T(8,128)(2,1)S(1)}, u32[]{:S(2)}, u32[]{:S(2)}) collective-permute-start(bf16[768,2048]{1,0:T(8,128)(2,1)} %param.1), channel_id=1, source_target_pairs={{1,0},{2,1},{3,2},{0,3},{5,4},{6,5},{7,6},{4,7},{9,8},{10,9},{11,1... | collective-permute-start | bytes 9437192 | tf_op jit(solution)/shard_map/ppermute | solution.py:26
  7.2 70.2 %collective-permute-start.1 = (bf16[768,2048]{1,0:T(8,128)(2,1)}, bf16[768,2048]{1,0:T(8,128)(2,1)}, u32[]{:S(2)}, u32[]{:S(2)}) collective-permute-start(bf16[768,2048]{1,0:T(8,128)(2,1)} %param.1), channel_id=1, source_target_pairs={{2,0},{3,1},{0,2},{1,3},{6,4},{7,5},{4,6},{5,7},{10,8},{11,9},{8,1... | collective-permute-start | bytes 9437192 | tf_op jit(solution)/shard_map/ppermute | solution.py:26
  7.4 70.0 %copy-start = (bf16[768,2048]{1,0:T(8,128)(2,1)S(1)}, bf16[768,2048]{1,0:T(8,128)(2,1)}, u32[]{:S(2)}) copy-start(bf16[768,2048]{1,0:T(8,128)(2,1)} %param.1) | copy-start | bytes 9437188
Sparse Core Ops, SparseCore 0:
  88.3 157.4 reduce-scatter.1
where the time goes:
time: 255 us; the launch traced here: 253 us
  waiting for transfers between devices  222 us (87%)
  between operations  13.4 us (5%)
  matrix products  12.8 us (5%)
  other arithmetic  3.55 us (1%)
    reduce_scatter x1, waiting for transfers between devices, local_fn(): result = lax.psum_scatter(result, 'kk', scatter_dimension=1, tiled=True)  158 us
    ppermute x2, waiting for transfers between devices, fetch_block(): return lax.ppermute(a_blk, 'g', perm_pairs)  64.4 us
    dot_general x1, matrix products, local_fn(): jnp.einsum('jrk,isk->jirs', big_stack, small_stack, preferred_element_typ...  7.13 us
    dot_general x1, matrix products, local_fn(): lax.dot_general(a_blk, a_blk, (((1,), (1,)), ((), ())), preferred_element...  5.62 us
  transfers between devices with their start and end apart: 3, of which 3 were waited for; matrix products, arithmetic and copies ran while one was open for 2% of the time, Pallas kernels for 0%

commit v1 on v0

v1 whole, which is shorter than its diff:
```python
import jax
import jax.numpy as jnp
from jax import lax
from jax.experimental import pallas as pl
from jax.experimental.pallas import tpu as pltpu
from jax.sharding import PartitionSpec as P

MESH = pl.DeviceIdType.MESH
NZ = 4
NG = 4


def kernel(a_hbm, out_hbm, abuf, part, ring, fin, load_sem, a_send, a_recv, f_send,
           z_send, z_recv, t_send, t_recv, o_sem):
    z = lax.axis_index("kk")
    g = lax.axis_index("g")
    rows = a_hbm.shape[0]
    qr = rows // NZ
    side = z // 2
    inner = ((z + 1) // 2) % 2
    has3 = ((g + 1) // 2) % 2
    toward = z + 1 - 2 * side
    away = z - 1 + 2 * side

    def mirror(q):
        return q + side * (3 - 2 * q)

    def order(i):
        return mirror(3 - i + inner * (i // 2) * (2 * i - 5))

    bar = pltpu.get_barrier_semaphore()
    for d in range(1, NG):
        pl.semaphore_signal(bar, inc=1, device_id={"g": (g + d) % NG}, device_id_type=MESH)
    pl.semaphore_signal(bar, inc=1, device_id={"kk": toward}, device_id_type=MESH)

    @pl.when(inner == 1)
    def _():
        pl.semaphore_signal(bar, inc=1, device_id={"kk": away}, device_id_type=MESH)

    load = pltpu.make_async_copy(a_hbm, abuf.at[0], load_sem)
    load.start()
    pl.semaphore_wait(bar, NG + inner)

    def chunk(q):
        return pl.ds(pl.multiple_of(q * qr, qr), qr)

    own_slot = 1 + g // 3

    def own_copy(q):
        return pltpu.make_async_remote_copy(
            a_hbm.at[chunk(q)], abuf.at[own_slot, chunk(q)], a_send.at[q], a_recv.at[own_slot - 1, q],
            device_id={"g": (g + NG - 1) % NG}, device_id_type=MESH)

    def arrival(slot, q):
        return pltpu.make_async_remote_copy(
            a_hbm.at[chunk(q)], abuf.at[slot, chunk(q)], a_send.at[q], a_recv.at[slot - 1, q],
            device_id={"g": (g + NG - 1) % NG}, device_id_type=MESH)

    fwd_slot = 4 - g

    def forward(q):
        s = jnp.clip(fwd_slot, 1, 2)
        return pltpu.make_async_remote_copy(
            abuf.at[s, chunk(q)], abuf.at[s, chunk(q)], f_send.at[q], a_recv.at[s - 1, q],
            device_id={"g": (g + NG - 1) % NG}, device_id_type=MESH)

    @pl.loop(0, NZ)
    def _(i):
        own_copy(order(i)).start()

    def product(b, q):
        if b == 0:
            left, right = 0, 0
        elif b == 1:
            two = (g // 2) * (1 - g % 2)
            left, right = 1 - two, two
        else:
            left, right = 2, 0
        part[b, q] = lax.dot_general(abuf[left, chunk(q)], abuf[right], (((1,), (1,)), ((), ())),
                                     preferred_element_type=jnp.float32)

    def z_copy(src, d, b, q, dev):
        return pltpu.make_async_remote_copy(
            src, ring.at[d, b, q], z_send.at[d, b, q], z_recv.at[d, b, q],
            device_id={"kk": dev}, device_id_type=MESH)

    def compute(b):
        if b == 1:
            @pl.when(g == 2)
            def _():
                for q in range(NZ):
                    arrival(1, q).wait_recv()

        @pl.loop(0, NZ)
        def _(i):
            q = order(i)
            if b == 1:
                @pl.when(g != 2)
                def _():
                    arrival(1, q).wait_recv()

                @pl.when(g == 3)
                def _():
                    forward(q).start()
            if b == 2:
                @pl.when(g == 1)
                def _():
                    arrival(2, q).wait_recv()
            product(b, q)

            @pl.when((inner == 0) & (i < 3))
            def _():
                z_copy(part.at[b, q], side, b, q, toward).start()

    def add_in(d, b, q):
        @pl.loop(0, qr // 16)
        def _(r):
            rs = pl.ds(pl.multiple_of(r * 16, 16), 16)
            ring[d, b, q, rs] = ring[d, b, q, rs] + part[b, q, rs]

    def wait_in(d, b, q):
        z_copy(ring.at[d, b, q], d, b, q, toward).wait_recv()

    def group1(b):
        @pl.when(inner == 1)
        def _():
            for mq in (3, 2):
                q = mirror(mq)
                wait_in(side, b, q)
                add_in(side, b, q)
                z_copy(ring.at[side, b, q], side, b, q, toward).start()
            q = mirror(0)
            wait_in(1 - side, b, q)
            add_in(1 - side, b, q)
            z_copy(ring.at[1 - side, b, q], 1 - side, b, q, away).start()

    def final(d, b, q):
        @pl.loop(0, qr // 16)
        def _(r):
            rs = pl.ds(pl.multiple_of(r * 16, 16), 16)
            fin[b, rs] = ring[d, b, q, rs] + part[b, q, rs]

    def out_copy(src, slot):
        return pltpu.make_async_copy(fin.at[src], out_hbm.at[slot], o_sem.at[slot])

    def hand_over():
        return pltpu.make_async_remote_copy(
            fin.at[1], fin.at[2], t_send, t_recv, device_id={"g": (g + 2) % NG}, device_id_type=MESH)

    def group2(b):
        @pl.when(inner == 1)
        def _():
            q = mirror(1)
            wait_in(side, b, q)
            add_in(side, b, q)
            wait_in(1 - side, b, q)

            @pl.loop(0, qr // 16)
            def _(r):
                rs = pl.ds(pl.multiple_of(r * 16, 16), 16)
                fin[b, rs] = ring[1 - side, b, q, rs] + ring[side, b, q, rs]

        @pl.when(inner == 0)
        def _():
            q = mirror(0)
            wait_in(1 - side, b, q)
            final(1 - side, b, q)

        if b == 0:
            out_copy(0, 0).start()
        elif b == 1:
            @pl.when(g != 2)
            def _():
                out_copy(1, 1).start()

            @pl.when(g == 2)
            def _():
                hand_over().start()
        else:
            out_copy(2, 3 - g).start()

    load.wait()
    compute(0)

    @pl.when(g >= 2)
    def _():
        @pl.loop(0, qr // 16)
        def _(r):
            fin[3, pl.ds(pl.multiple_of(r * 16, 16), 16)] = jnp.zeros((16, rows), jnp.float32)
        out_copy(3, 2).start()

    @pl.when(g == 2)
    def _():
        @pl.loop(0, NZ)
        def _(i):
            q = order(i)
            arrival(2, q).wait_recv()
            forward(q).start()

    group1(0)
    compute(1)
    group2(0)
    group1(1)

    @pl.when(has3 == 1)
    def _():
        compute(2)

    group2(1)

    @pl.when(has3 == 1)
    def _():
        group1(2)
        group2(2)

    @pl.when(g == 0)
    def _():
        hand_over().wait_recv()
        out_copy(2, 2).start()

    @pl.loop(0, NZ)
    def _(q):
        own_copy(q).wait_send()

    @pl.when(g >= 2)
    def _():
        @pl.loop(0, NZ)
        def _(q):
            forward(q).wait_send()

    @pl.when(g == 2)
    def _():
        hand_over().wait_send()

    def drain(b):
        @pl.when(inner == 0)
        def _():
            for mq in (3, 2, 1):
                q = mirror(mq)
                z_copy(part.at[b, q], side, b, q, toward).wait_send()

        @pl.when(inner == 1)
        def _():
            for mq in (3, 2):
                q = mirror(mq)
                z_copy(ring.at[side, b, q], side, b, q, toward).wait_send()
            q = mirror(0)
            z_copy(ring.at[1 - side, b, q], 1 - side, b, q, away).wait_send()

    drain(0)
    drain(1)

    @pl.when(has3 == 1)
    def _():
        drain(2)

    for s in range(3):
        out_copy(s, s).wait()


def solution(mesh):
    def local_fn(a_blk):
        rows, cols = a_blk.shape
        qr = rows // NZ
        dma = pltpu.SemaphoreType.DMA
        out = pl.pallas_call(
            kernel,
            out_shape=jax.ShapeDtypeStruct((3, qr, rows), jnp.float32),
            in_specs=[pl.BlockSpec(memory_space=pl.ANY)],
            out_specs=pl.BlockSpec(memory_space=pl.ANY),
            scratch_shapes=[
                pltpu.VMEM((3, rows, cols), jnp.bfloat16),
                pltpu.VMEM((3, NZ, qr, rows), jnp.float32),
                pltpu.VMEM((2, 3, NZ, qr, rows), jnp.float32),
                pltpu.VMEM((4, qr, rows), jnp.float32),
                dma, dma((NZ,)), dma((2, NZ)), dma((NZ,)),
                dma((2, 3, NZ)), dma((2, 3, NZ)), dma, dma, dma((3,)),
            ],
            compiler_params=pltpu.CompilerParams(
                collective_id=0, has_side_effects=True, vmem_limit_bytes=56 * 2**20),
        )(a_blk)
        return out[None]

    return jax.shard_map(local_fn, mesh=mesh, in_specs=(P(("m", "g"), "kk"),),
                         out_specs=P(("m", "g"), None, "kk", None), check_vma=False)
```

time: 255 us -> 111 us (0.44)
  the two profiles are of different devices: /device:TPU:21 before, /device:TPU:4 now
where the time goes in v1:
time: 111 us
  Pallas kernels  108 us (97%)
  local copies, waits for them, and re-layouts  2.8 us (3%)
    pallas_call x1, Pallas kernels, local_fn(): pl.pallas_call(kernel, out_shape=jax.ShapeDtypeStruct((3, qr, rows), jnp....  108 us
    unnamed x1, local copies, waits for them, and re-layouts  2.8 us

profile of v1, /device:TPU:4, one launch (start us, length us, event | category | flops | bytes accessed | tf_op | source)
XLA Modules:
  0.0 110.9 jit_solution(6151277554564222985)
XLA Ops:
  0.0 108.1 %shard_map.17 = f32[3,192,768]{2,1,0:T(8,128)} custom-call(bf16[768,2048]{1,0:T(8,128)(2,1)} %a_hbm.1), custom_call_target="tpu_custom_call" | custom-call | tf_op jit(solution)/shard_map/pallas_call | solution.py:266
  108.1 2.8 %copy.3 = f32[1,3,192,768]{3,2,1,0:T(8,128)} copy(f32[1,3,192,768]{3,2,1,0:T(8,128)} %bitcast.1) | data formatting | bytes 3538944

commit v2 on v1

--- a/solution.py
+++ b/solution.py
@@ -8,6 +8,7 @@
 MESH = pl.DeviceIdType.MESH
 NZ = 4
 NG = 4
+SENT = {3: 768, 2: 640, 1: 384}
 
 
 def kernel(a_hbm, out_hbm, abuf, part, ring, fin, load_sem, a_send, a_recv, f_send,
@@ -79,10 +80,33 @@
         part[b, q] = lax.dot_general(abuf[left, chunk(q)], abuf[right], (((1,), (1,)), ((), ())),
                                      preferred_element_type=jnp.float32)
 
-    def z_copy(src, d, b, q, dev):
-        return pltpu.make_async_remote_copy(
-            src, ring.at[d, b, q], z_send.at[d, b, q], z_recv.at[d, b, q],
+    half = qr // 2
+
+    def part_of(b, d, mq, h):
+        rs = pl.ds(h * half, half)
+        size = rows if b else SENT[mq]
+        start = d * (rows - size)
+        return rs, pl.ds(pl.multiple_of(start, 128), size)
+
+    def z_copy(src, b, d, mq, q, h, dev):
+        rs, cs = part_of(b, d, mq, h)
+        return pltpu.make_async_remote_copy(
+            src.at[q, rs, cs], ring.at[d, b, q, rs, cs],
+            z_send.at[d, b, q, h], z_recv.at[d, b, q, h],
             device_id={"kk": dev}, device_id_type=MESH)
+
+    def near_send(src, b, mq, h):
+        return z_copy(src, b, side, mq, mirror(mq), h, toward)
+
+    def far_send(b, h):
+        return z_copy(ring.at[1 - side, b], b, 1 - side, 3, mirror(0), h, away)
+
+    def wait_near(b, mq, h):
+        near_send(ring.at[side, b], b, mq, h).wait_recv()
+
+    def wait_far(b, mq, h):
+        d = 1 - side
+        z_copy(ring.at[d, b], b, d, 3 - mq, mirror(mq), h, toward).wait_recv()
 
     def compute(b):
         if b == 1:
@@ -108,37 +132,32 @@
                     arrival(2, q).wait_recv()
             product(b, q)
 
-            @pl.when((inner == 0) & (i < 3))
-            def _():
-                z_copy(part.at[b, q], side, b, q, toward).start()
-
-    def add_in(d, b, q):
-        @pl.loop(0, qr // 16)
+            for k in range(3):
+                @pl.when((inner == 0) & (i == k))
+                def _():
+                    for h in range(2):
+                        near_send(part.at[b], b, 3 - k, h).start()
+
+    def add_in(b, d, mq, q, h):
+        _, cs = part_of(b, d, mq, h)
+
+        @pl.loop(0, half // 16)
         def _(r):
-            rs = pl.ds(pl.multiple_of(r * 16, 16), 16)
-            ring[d, b, q, rs] = ring[d, b, q, rs] + part[b, q, rs]
-
-    def wait_in(d, b, q):
-        z_copy(ring.at[d, b, q], d, b, q, toward).wait_recv()
+            rs = pl.ds(pl.multiple_of(h * half + r * 16, 16), 16)
+            ring[d, b, q, rs, cs] = ring[d, b, q, rs, cs] + part[b, q, rs, cs]
 
     def group1(b):
         @pl.when(inner == 1)
         def _():
-            for mq in (3, 2):
-                q = mirror(mq)
-                wait_in(side, b, q)
-                add_in(side, b, q)
-                z_copy(ring.at[side, b, q], side, b, q, toward).start()
-            q = mirror(0)
-            wait_in(1 - side, b, q)
-            add_in(1 - side, b, q)
-            z_copy(ring.at[1 - side, b, q], 1 - side, b, q, away).start()
-
-    def final(d, b, q):
-        @pl.loop(0, qr // 16)
-        def _(r):
-            rs = pl.ds(pl.multiple_of(r * 16, 16), 16)
-            fin[b, rs] = ring[d, b, q, rs] + part[b, q, rs]
+            for mq, h in ((3, 0), (3, 1), (0, 0), (2, 0), (0, 1), (2, 1)):
+                if mq:
+                    wait_near(b, mq, h)
+                    add_in(b, side, mq, mirror(mq), h)
+                    near_send(ring.at[side, b], b, mq, h).start()
+                else:
+                    wait_far(b, 0, h)
+                    add_in(b, 1 - side, 3, mirror(0), h)
+                    far_send(b, h).start()
 
     def out_copy(src, slot):
         return pltpu.make_async_copy(fin.at[src], out_hbm.at[slot], o_sem.at[slot])
@@ -151,20 +170,45 @@
         @pl.when(inner == 1)
         def _():
             q = mirror(1)
-            wait_in(side, b, q)
-            add_in(side, b, q)
-            wait_in(1 - side, b, q)
-
-            @pl.loop(0, qr // 16)
-            def _(r):
-                rs = pl.ds(pl.multiple_of(r * 16, 16), 16)
-                fin[b, rs] = ring[1 - side, b, q, rs] + ring[side, b, q, rs]
+            for h in range(2):
+                wait_far(b, 1, h)
+                wait_near(b, 1, h)
+                if b:
+                    @pl.loop(0, half // 16)
+                    def _(r):
+                        rs = pl.ds(pl.multiple_of(h * half + r * 16, 16), 16)
+                        fin[b, rs] = ring[0, b, q, rs] + part[b, q, rs] + ring[1, b, q, rs]
+
+        if b == 0:
+            one, mid = SENT[2], SENT[1]
+            lo = rows - one
+
+            @pl.when(z == 1)
+            def _():
+                turned = ring[1, 0, 0, 0:lo, lo:mid].T
+                fin[0, :, 0:lo] = ring[0, 0, 1, :, 0:lo] + turned[mid - lo - qr:]
+                fin[0, :, lo:mid] = ring[0, 0, 1, :, lo:mid] + part[0, 1, :, lo:mid] + ring[1, 0, 1, :, lo:mid]
+                turned = jnp.concatenate([ring[0, 0, 2, :, lo:mid], ring[0, 0, 3, :, lo:mid]], axis=0).T
+                fin[0, :, mid:] = ring[1, 0, 1, :, mid:] + turned[mid - lo - qr:]
+
+            @pl.when(z == 2)
+            def _():
+                turned = ring[0, 0, 3, qr - lo:, mid:one].T
+                fin[0, :, one:] = ring[1, 0, 2, :, one:] + turned[:qr]
+                fin[0, :, mid:one] = ring[0, 0, 2, :, mid:one] + part[0, 2, :, mid:one] + ring[1, 0, 2, :, mid:one]
+                turned = jnp.concatenate([ring[1, 0, 0, :, mid:one], ring[1, 0, 1, :, mid:one]], axis=0).T
+                fin[0, :, :mid] = ring[0, 0, 2, :, :mid] + turned[:qr]
 
         @pl.when(inner == 0)
         def _():
             q = mirror(0)
-            wait_in(1 - side, b, q)
-            final(1 - side, b, q)
+            for h in range(2):
+                wait_far(b, 0, h)
+
+                @pl.loop(0, half // 16)
+                def _(r):
+                    rs = pl.ds(pl.multiple_of(h * half + r * 16, 16), 16)
+                    fin[b, rs] = ring[1 - side, b, q, rs] + part[b, q, rs]
 
         if b == 0:
             out_copy(0, 0).start()
@@ -233,19 +277,17 @@
         hand_over().wait_send()
 
     def drain(b):
-        @pl.when(inner == 0)
-        def _():
-            for mq in (3, 2, 1):
-                q = mirror(mq)
-                z_copy(part.at[b, q], side, b, q, toward).wait_send()
-
-        @pl.when(inner == 1)
-        def _():
-            for mq in (3, 2):
-                q = mirror(mq)
-                z_copy(ring.at[side, b, q], side, b, q, toward).wait_send()
-            q = mirror(0)
-            z_copy(ring.at[1 - side, b, q], 1 - side, b, q, away).wait_send()
+        for h in range(2):
+            @pl.when(inner == 0)
+            def _():
+                for mq in (3, 2, 1):
+                    near_send(part.at[b], b, mq, h).wait_send()
+
+            @pl.when(inner == 1)
+            def _():
+                for mq in (3, 2):
+                    near_send(ring.at[side, b], b, mq, h).wait_send()
+                far_send(b, h).wait_send()
 
     drain(0)
     drain(1)
@@ -274,7 +316,7 @@
                 pltpu.VMEM((2, 3, NZ, qr, rows), jnp.float32),
                 pltpu.VMEM((4, qr, rows), jnp.float32),
                 dma, dma((NZ,)), dma((2, NZ)), dma((NZ,)),
-                dma((2, 3, NZ)), dma((2, 3, NZ)), dma, dma, dma((3,)),
+                dma((2, 3, NZ, 2)), dma((2, 3, NZ, 2)), dma, dma, dma((3,)),
             ],
             compiler_params=pltpu.CompilerParams(
                 collective_id=0, has_side_effects=True, vmem_limit_bytes=56 * 2**20),

time: 111 us -> 96.6 us (0.87)
  the two profiles are of different devices: /device:TPU:4 before, /device:TPU:19 now
where the time goes in v2:
time: 96.6 us; the launch traced here: 96.5 us
  Pallas kernels  93.7 us (97%)
  local copies, waits for them, and re-layouts  2.8 us (3%)
    pallas_call x1, Pallas kernels, local_fn(): pl.pallas_call(kernel, out_shape=jax.ShapeDtypeStruct((3, qr, rows), jnp....  93.7 us
    unnamed x1, local copies, waits for them, and re-layouts  2.8 us

profile of v2, /device:TPU:19, one launch (start us, length us, event | category | flops | bytes accessed | tf_op | source)
XLA Modules:
  0.0 96.5 jit_solution(6410952550643957400)
XLA Ops:
  0.0 93.7 %shard_map.17 = f32[3,192,768]{2,1,0:T(8,128)} custom-call(bf16[768,2048]{1,0:T(8,128)(2,1)} %a_hbm.1), custom_call_target="tpu_custom_call" | custom-call | tf_op jit(solution)/shard_map/pallas_call | solution.py:308
  93.7 2.8 %copy.3 = f32[1,3,192,768]{3,2,1,0:T(8,128)} copy(f32[1,3,192,768]{3,2,1,0:T(8,128)} %bitcast.1) | data formatting | bytes 3538944

commit v3 on v2

--- a/solution.py
+++ b/solution.py
@@ -11,8 +11,8 @@
 SENT = {3: 768, 2: 640, 1: 384}
 
 
-def kernel(a_hbm, out_hbm, abuf, part, ring, fin, load_sem, a_send, a_recv, f_send,
-           z_send, z_recv, t_send, t_recv, o_sem):
+def kernel(a_hbm, out, abuf, part, ring, got, load_sem, a_send, a_recv, f_send,
+           z_send, z_recv, t_send, t_recv):
     z = lax.axis_index("kk")
     g = lax.axis_index("g")
     rows = a_hbm.shape[0]
@@ -159,14 +159,14 @@
                     add_in(b, 1 - side, 3, mirror(0), h)
                     far_send(b, h).start()
 
-    def out_copy(src, slot):
-        return pltpu.make_async_copy(fin.at[src], out_hbm.at[slot], o_sem.at[slot])
-
     def hand_over():
         return pltpu.make_async_remote_copy(
-            fin.at[1], fin.at[2], t_send, t_recv, device_id={"g": (g + 2) % NG}, device_id_type=MESH)
+            out.at[2], got, t_send, t_recv, device_id={"g": (g + 2) % NG}, device_id_type=MESH)
 
     def group2(b):
+        two = (g // 2) * (1 - g % 2)
+        slot = (0, 1 + two, 3 - g)[b]
+
         @pl.when(inner == 1)
         def _():
             q = mirror(1)
@@ -177,7 +177,7 @@
                     @pl.loop(0, half // 16)
                     def _(r):
                         rs = pl.ds(pl.multiple_of(h * half + r * 16, 16), 16)
-                        fin[b, rs] = ring[0, b, q, rs] + part[b, q, rs] + ring[1, b, q, rs]
+                        out[slot, rs] = ring[0, b, q, rs] + part[b, q, rs] + ring[1, b, q, rs]
 
         if b == 0:
             one, mid = SENT[2], SENT[1]
@@ -186,18 +186,18 @@
             @pl.when(z == 1)
             def _():
                 turned = ring[1, 0, 0, 0:lo, lo:mid].T
-                fin[0, :, 0:lo] = ring[0, 0, 1, :, 0:lo] + turned[mid - lo - qr:]
-                fin[0, :, lo:mid] = ring[0, 0, 1, :, lo:mid] + part[0, 1, :, lo:mid] + ring[1, 0, 1, :, lo:mid]
+                out[0, :, 0:lo] = ring[0, 0, 1, :, 0:lo] + turned[mid - lo - qr:]
+                out[0, :, lo:mid] = ring[0, 0, 1, :, lo:mid] + part[0, 1, :, lo:mid] + ring[1, 0, 1, :, lo:mid]
                 turned = jnp.concatenate([ring[0, 0, 2, :, lo:mid], ring[0, 0, 3, :, lo:mid]], axis=0).T
-                fin[0, :, mid:] = ring[1, 0, 1, :, mid:] + turned[mid - lo - qr:]
+                out[0, :, mid:] = ring[1, 0, 1, :, mid:] + turned[mid - lo - qr:]
 
             @pl.when(z == 2)
             def _():
                 turned = ring[0, 0, 3, qr - lo:, mid:one].T
-                fin[0, :, one:] = ring[1, 0, 2, :, one:] + turned[:qr]
-                fin[0, :, mid:one] = ring[0, 0, 2, :, mid:one] + part[0, 2, :, mid:one] + ring[1, 0, 2, :, mid:one]
+                out[0, :, one:] = ring[1, 0, 2, :, one:] + turned[:qr]
+                out[0, :, mid:one] = ring[0, 0, 2, :, mid:one] + part[0, 2, :, mid:one] + ring[1, 0, 2, :, mid:one]
                 turned = jnp.concatenate([ring[1, 0, 0, :, mid:one], ring[1, 0, 1, :, mid:one]], axis=0).T
-                fin[0, :, :mid] = ring[0, 0, 2, :, :mid] + turned[:qr]
+                out[0, :, :mid] = ring[0, 0, 2, :, :mid] + turned[:qr]
 
         @pl.when(inner == 0)
         def _():
@@ -208,30 +208,21 @@
                 @pl.loop(0, half // 16)
                 def _(r):
                     rs = pl.ds(pl.multiple_of(h * half + r * 16, 16), 16)
-                    fin[b, rs] = ring[1 - side, b, q, rs] + part[b, q, rs]
-
-        if b == 0:
-            out_copy(0, 0).start()
-        elif b == 1:
-            @pl.when(g != 2)
-            def _():
-                out_copy(1, 1).start()
-
+                    out[slot, rs] = ring[1 - side, b, q, rs] + part[b, q, rs]
+
+        if b == 1:
             @pl.when(g == 2)
             def _():
                 hand_over().start()
-        else:
-            out_copy(2, 3 - g).start()
+
+    def fill(value):
+        @pl.loop(0, qr // 16)
+        def _(r):
+            rs = pl.ds(pl.multiple_of(r * 16, 16), 16)
+            out[2, rs] = value(rs)
 
     load.wait()
     compute(0)
-
-    @pl.when(g >= 2)
-    def _():
-        @pl.loop(0, qr // 16)
-        def _(r):
-            fin[3, pl.ds(pl.multiple_of(r * 16, 16), 16)] = jnp.zeros((16, rows), jnp.float32)
-        out_copy(3, 2).start()
 
     @pl.when(g == 2)
     def _():
@@ -260,7 +251,7 @@
     @pl.when(g == 0)
     def _():
         hand_over().wait_recv()
-        out_copy(2, 2).start()
+        fill(lambda rs: got[rs])
 
     @pl.loop(0, NZ)
     def _(q):
@@ -276,6 +267,10 @@
     def _():
         hand_over().wait_send()
 
+    @pl.when(g >= 2)
+    def _():
+        fill(lambda rs: jnp.zeros((16, rows), jnp.float32))
+
     def drain(b):
         for h in range(2):
             @pl.when(inner == 0)
@@ -295,9 +290,6 @@
     @pl.when(has3 == 1)
     def _():
         drain(2)
-
-    for s in range(3):
-        out_copy(s, s).wait()
 
 
 def solution(mesh):
@@ -308,18 +300,18 @@
         out = pl.pallas_call(
             kernel,
             out_shape=jax.ShapeDtypeStruct((3, qr, rows), jnp.float32),
-            in_specs=[pl.BlockSpec(memory_space=pl.ANY)],
-            out_specs=pl.BlockSpec(memory_space=pl.ANY),
+            in_specs=[pl.BlockSpec(memory_space=pltpu.HBM)],
+            out_specs=pl.BlockSpec(memory_space=pltpu.VMEM),
             scratch_shapes=[
                 pltpu.VMEM((3, rows, cols), jnp.bfloat16),
                 pltpu.VMEM((3, NZ, qr, rows), jnp.float32),
                 pltpu.VMEM((2, 3, NZ, qr, rows), jnp.float32),
-                pltpu.VMEM((4, qr, rows), jnp.float32),
+                pltpu.VMEM((qr, rows), jnp.float32),
                 dma, dma((NZ,)), dma((2, NZ)), dma((NZ,)),
-                dma((2, 3, NZ, 2)), dma((2, 3, NZ, 2)), dma, dma, dma((3,)),
+                dma((2, 3, NZ, 2)), dma((2, 3, NZ, 2)), dma, dma,
             ],
             compiler_params=pltpu.CompilerParams(
-                collective_id=0, has_side_effects=True, vmem_limit_bytes=56 * 2**20),
+                collective_id=0, has_side_effects=True, vmem_limit_bytes=50 * 2**20),
         )(a_blk)
         return out[None]
 

time: 96.6 us -> 94.4 us (0.977)
  the two profiles are of different devices: /device:TPU:19 before, /device:TPU:12 now
where the time goes in v3:
time: 94.4 us; the launch traced here: 94.2 us
  Pallas kernels  93 us (99%)
  local copies, waits for them, and re-layouts  1.21 us (1%)
    pallas_call x1, Pallas kernels, local_fn(): pl.pallas_call(kernel, out_shape=jax.ShapeDtypeStruct((3, qr, rows), jnp....  93 us

profile of v3, /device:TPU:12, one launch (start us, length us, event | category | flops | bytes accessed | tf_op | source)
XLA Modules:
  0.0 94.2 jit_solution(1033075414255662481)
XLA Ops:
  0.0 93.0 %shard_map.17 = f32[3,192,768]{2,1,0:T(8,128)S(1)} custom-call(bf16[768,2048]{1,0:T(8,128)(2,1)} %a_hbm.1), custom_call_target="tpu_custom_call" | custom-call | tf_op jit(solution)/shard_map/pallas_call | solution.py:300
  93.0 1.2 %copy.3 = f32[1,3,192,768]{3,2,1,0:T(8,128)} copy(f32[1,3,192,768]{3,2,1,0:T(8,128)S(1)} %bitcast.1) | data formatting | bytes 3538944

commit v4 on v3

v4 whole, which is shorter than its diff:
```python
import jax
import jax.numpy as jnp
from jax import lax
from jax.experimental import pallas as pl
from jax.experimental.pallas import tpu as pltpu
from jax.sharding import PartitionSpec as P

MESH = pl.DeviceIdType.MESH
NZ = 4
NG = 4
SENT = {3: 768, 2: 640, 1: 384}


def kernel(a_hbm, out, abuf, part, ring, got, load_sem, a_send, u_send, f_send, a_recv,
           z_send, z_recv, t_send, t_recv):
    z = lax.axis_index("kk")
    g = lax.axis_index("g")
    rows = a_hbm.shape[0]
    qr = rows // NZ
    side = z // 2
    inner = ((z + 1) // 2) % 2
    has3 = g % 2
    last = g // 3
    toward = z + 1 - 2 * side
    away = z - 1 + 2 * side

    def mirror(q):
        return q + side * (3 - 2 * q)

    def order(i):
        return mirror(3 - i + inner * (i // 2) * (2 * i - 5))

    def third(k, d):
        return pl.ds(pl.multiple_of((2 - k + d * (2 * k - 2)) * (rows // 3), rows // 3), rows // 3)

    def load(k):
        return pltpu.make_async_copy(a_hbm.at[third(k, side)], abuf.at[0, third(k, side)], load_sem.at[k])

    for k in range(3):
        load(k).start()

    bar = pltpu.get_barrier_semaphore()
    for d in (1, NG - 1):
        pl.semaphore_signal(bar, inc=1, device_id={"g": (g + d) % NG}, device_id_type=MESH)
    pl.semaphore_signal(bar, inc=1, device_id={"kk": toward}, device_id_type=MESH)

    @pl.when(inner == 1)
    def _():
        pl.semaphore_signal(bar, inc=1, device_id={"kk": away}, device_id_type=MESH)

    def chunk(q):
        return pl.ds(pl.multiple_of(q * qr, qr), qr)

    def row_copy(src, slot, q, d, send):
        return pltpu.make_async_remote_copy(
            src.at[chunk(q)], abuf.at[slot, chunk(q)], send.at[q], a_recv.at[slot - 1, q],
            device_id={"g": (g + d) % NG}, device_id_type=MESH)

    def own_copy(q):
        return row_copy(a_hbm, 1, q, NG - 1, a_send)

    def own_copy_up(q):
        return row_copy(a_hbm, 2, q, 1, u_send)

    def forward(q):
        return row_copy(abuf.at[1], 2, q, NG - 1, f_send)

    def arrival(slot, q):
        return row_copy(a_hbm, slot, q, NG - 1, a_send)

    def product(b, q):
        left = (0, 1 + last, 2 - last)[b]
        right = (0, last, 0)[b]
        part[b, q] = lax.dot_general(abuf[left, chunk(q)], abuf[right], (((1,), (1,)), ((), ())),
                                     preferred_element_type=jnp.float32)

    def product_third(q, k):
        load(k).wait()
        part[0, q, :, third(k, side)] = lax.dot_general(
            abuf[0, chunk(q)], abuf[0, third(k, side)], (((1,), (1,)), ((), ())),
            preferred_element_type=jnp.float32)

    half = qr // 2

    def pieces(b, mq):
        return 3 if b == 0 and mq == 3 else 2

    def part_of(b, d, mq, h):
        if pieces(b, mq) == 3:
            return pl.ds(0, qr), third(h, d)
        rs = pl.ds(h * half, half)
        size = rows if b else SENT[mq]
        start = d * (rows - size)
        return rs, pl.ds(pl.multiple_of(start, 128), size)

    def z_copy(src, b, d, mq, q, h, dev):
        rs, cs = part_of(b, d, mq, h)
        return pltpu.make_async_remote_copy(
            src.at[q, rs, cs], ring.at[d, b, q, rs, cs],
            z_send.at[d, b, q, h], z_recv.at[d, b, q, h],
            device_id={"kk": dev}, device_id_type=MESH)

    def near_send(src, b, mq, h):
        return z_copy(src, b, side, mq, mirror(mq), h, toward)

    def far_send(b, h):
        return z_copy(ring.at[1 - side, b], b, 1 - side, 3, mirror(0), h, away)

    def wait_near(b, mq, h):
        near_send(ring.at[side, b], b, mq, h).wait_recv()

    def wait_far(b, mq, h):
        d = 1 - side
        z_copy(ring.at[d, b], b, d, 3 - mq, mirror(mq), h, toward).wait_recv()

    def compute(b):
        def step(i):
            q = order(i)
            if b == 1:
                @pl.when(last == 0)
                def _():
                    arrival(1, q).wait_recv()

                @pl.when(g == 2)
                def _():
                    forward(q).start()

                @pl.when(last == 1)
                def _():
                    arrival(2, q).wait_recv()
            if b == 2:
                @pl.when(g == 1)
                def _():
                    arrival(2, q).wait_recv()
            product(b, q)
            for k in range(3):
                @pl.when((inner == 0) & (i == k))
                def _():
                    for h in range(pieces(b, 3 - k)):
                        near_send(part.at[b], b, 3 - k, h).start()

        if b == 1:
            @pl.when(last == 1)
            def _():
                for q in range(NZ):
                    arrival(1, q).wait_recv()
        pl.loop(0 if b else 1, NZ)(step)

    def start():
        q = order(0)
        for k in range(3):
            product_third(q, k)
            if k == 0:
                pl.semaphore_wait(bar, 3 + inner)

            @pl.when(inner == 0)
            def _():
                near_send(part.at[0], 0, 3, k).start()
            if k == 0:
                @pl.loop(0, NZ)
                def _(i):
                    own_copy(order(i)).start()

                @pl.when(g == 2)
                def _():
                    @pl.loop(0, NZ)
                    def _(i):
                        own_copy_up(order(i)).start()

    def row_loop(rs, body):
        @pl.loop(0, rs.size // 16)
        def _(r):
            body(pl.ds(pl.multiple_of(rs.start + r * 16, 16), 16))

    def add_in(b, d, mq, q, h):
        rs, cs = part_of(b, d, mq, h)

        def body(rr):
            ring[d, b, q, rr, cs] = ring[d, b, q, rr, cs] + part[b, q, rr, cs]
        row_loop(rs, body)

    def group1(b):
        if b == 0:
            turns = ((3, 0), (3, 1), (3, 2), (0, 0), (0, 1), (2, 0), (0, 2), (2, 1))
        else:
            turns = ((3, 0), (3, 1), (0, 0), (2, 0), (0, 1), (2, 1))

        @pl.when(inner == 1)
        def _():
            for mq, h in turns:
                if mq:
                    wait_near(b, mq, h)
                    add_in(b, side, mq, mirror(mq), h)
                    near_send(ring.at[side, b], b, mq, h).start()
                else:
                    wait_far(b, 0, h)
                    add_in(b, 1 - side, 3, mirror(0), h)
                    far_send(b, h).start()

    def hand_over():
        return pltpu.make_async_remote_copy(
            out.at[2], got, t_send, t_recv, device_id={"g": (g + 1) % NG}, device_id_type=MESH)

    def group2(b):
        slot = (0, 1 + last, (5 - g) // 2)[b]

        @pl.when(inner == 1)
        def _():
            q = mirror(1)
            for h in range(2):
                wait_far(b, 1, h)
                wait_near(b, 1, h)
                if b:
                    @pl.loop(0, half // 16)
                    def _(r):
                        rs = pl.ds(pl.multiple_of(h * half + r * 16, 16), 16)
                        out[slot, rs] = ring[0, b, q, rs] + part[b, q, rs] + ring[1, b, q, rs]

        if b == 0:
            one, mid = SENT[2], SENT[1]
            lo = rows - one

            @pl.when(z == 1)
            def _():
                turned = ring[1, 0, 0, 0:lo, lo:mid].T
                out[0, :, 0:lo] = ring[0, 0, 1, :, 0:lo] + turned[mid - lo - qr:]
                out[0, :, lo:mid] = ring[0, 0, 1, :, lo:mid] + part[0, 1, :, lo:mid] + ring[1, 0, 1, :, lo:mid]
                turned = jnp.concatenate([ring[0, 0, 2, :, lo:mid], ring[0, 0, 3, :, lo:mid]], axis=0).T
                out[0, :, mid:] = ring[1, 0, 1, :, mid:] + turned[mid - lo - qr:]

            @pl.when(z == 2)
            def _():
                turned = ring[0, 0, 3, qr - lo:, mid:one].T
                out[0, :, one:] = ring[1, 0, 2, :, one:] + turned[:qr]
                out[0, :, mid:one] = ring[0, 0, 2, :, mid:one] + part[0, 2, :, mid:one] + ring[1, 0, 2, :, mid:one]
                turned = jnp.concatenate([ring[1, 0, 0, :, mid:one], ring[1, 0, 1, :, mid:one]], axis=0).T
                out[0, :, :mid] = ring[0, 0, 2, :, :mid] + turned[:qr]

        @pl.when(inner == 0)
        def _():
            q = mirror(0)
            for h in range(pieces(b, 3)):
                wait_far(b, 0, h)
                rs, cs = part_of(b, 1 - side, 3, h)

                def body(rr):
                    out[slot, rr, cs] = ring[1 - side, b, q, rr, cs] + part[b, q, rr, cs]
                row_loop(rs, body)

        if b == 1:
            @pl.when(last == 1)
            def _():
                hand_over().start()

    def fill(value):
        @pl.loop(0, qr // 16)
        def _(r):
            rs = pl.ds(pl.multiple_of(r * 16, 16), 16)
            out[2, rs] = value(rs)

    start()
    compute(0)
    group1(0)
    compute(1)
    group2(0)
    group1(1)

    @pl.when(has3 == 1)
    def _():
        compute(2)

    group2(1)

    @pl.when(has3 == 1)
    def _():
        group1(2)
        group2(2)

    @pl.when(g == 0)
    def _():
        hand_over().wait_recv()
        fill(lambda rs: got[rs])

    @pl.loop(0, NZ)
    def _(q):
        own_copy(q).wait_send()

    @pl.when(g == 2)
    def _():
        @pl.loop(0, NZ)
        def _(q):
            own_copy_up(q).wait_send()
            forward(q).wait_send()

    @pl.when(last == 1)
    def _():
        hand_over().wait_send()

    @pl.when(g >= 2)
    def _():
        fill(lambda rs: jnp.zeros((16, rows), jnp.float32))

    def drain(b):
        @pl.when(inner == 0)
        def _():
            for mq in (3, 2, 1):
                for h in range(pieces(b, mq)):
                    near_send(part.at[b], b, mq, h).wait_send()

        @pl.when(inner == 1)
        def _():
            for mq in (3, 2):
                for h in range(pieces(b, mq)):
                    near_send(ring.at[side, b], b, mq, h).wait_send()
            for h in range(pieces(b, 3)):
                far_send(b, h).wait_send()

    drain(0)
    drain(1)

    @pl.when(has3 == 1)
    def _():
        drain(2)


def solution(mesh):
    def local_fn(a_blk):
        rows, cols = a_blk.shape
        qr = rows // NZ
        dma = pltpu.SemaphoreType.DMA
        out = pl.pallas_call(
            kernel,
            out_shape=jax.ShapeDtypeStruct((3, qr, rows), jnp.float32),
            in_specs=[pl.BlockSpec(memory_space=pltpu.HBM)],
            out_specs=pl.BlockSpec(memory_space=pltpu.VMEM),
            scratch_shapes=[
                pltpu.VMEM((3, rows, cols), jnp.bfloat16),
                pltpu.VMEM((3, NZ, qr, rows), jnp.float32),
                pltpu.VMEM((2, 3, NZ, qr, rows), jnp.float32),
                pltpu.VMEM((qr, rows), jnp.float32),
                dma((3,)), dma((NZ,)), dma((NZ,)), dma((NZ,)), dma((2, NZ)),
                dma((2, 3, NZ, 3)), dma((2, 3, NZ, 3)), dma, dma,
            ],
            compiler_params=pltpu.CompilerParams(
                collective_id=0, has_side_effects=True, vmem_limit_bytes=50 * 2**20),
        )(a_blk)
        return out[None]

    return jax.shard_map(local_fn, mesh=mesh, in_specs=(P(("m", "g"), "kk"),),
                         out_specs=P(("m", "g"), None, "kk", None), check_vma=False)
```

time: 94.4 us -> 93.5 us (level)
  the two profiles are of different devices: /device:TPU:12 before, /device:TPU:21 now
where the time goes in v4:
time: 93.5 us; the launch traced here: 93.3 us
  Pallas kernels  92.1 us (99%)
  local copies, waits for them, and re-layouts  1.21 us (1%)
    pallas_call x1, Pallas kernels, local_fn(): pl.pallas_call(kernel, out_shape=jax.ShapeDtypeStruct((3, qr, rows), jnp....  92.1 us

profile of v4, /device:TPU:21, one launch (start us, length us, event | category | flops | bytes accessed | tf_op | source)
XLA Modules:
  0.0 93.3 jit_solution(9915630807232384102)
XLA Ops:
  0.0 92.1 %shard_map.17 = f32[3,192,768]{2,1,0:T(8,128)S(1)} custom-call(bf16[768,2048]{1,0:T(8,128)(2,1)} %a_hbm.1), custom_call_target="tpu_custom_call" | custom-call | tf_op jit(solution)/shard_map/pallas_call | solution.py:331
  92.1 1.2 %copy.3 = f32[1,3,192,768]{3,2,1,0:T(8,128)} copy(f32[1,3,192,768]{3,2,1,0:T(8,128)S(1)} %bitcast.1) | data formatting | bytes 3538944

commit v5 on v4

v5 whole, which is shorter than its diff:
```python
import jax
import jax.numpy as jnp
from jax import lax
from jax.experimental import pallas as pl
from jax.experimental.pallas import tpu as pltpu
from jax.sharding import PartitionSpec as P

MESH = pl.DeviceIdType.MESH
NZ = 4
NG = 4
ROWS = 768
QR = ROWS // NZ
HALF = QR // 2
FIRST = 128
SENT = {3: 768, 2: 640, 1: 384}


def pieces(b, mq):
    return (1 if mq < 3 else 2) if b == 0 else 2


def near_index(b, mq, h):
    base = 0
    for k in range(b):
        base += sum(pieces(k, m) for m in (3, 2, 1)) + pieces(k, 3) + pieces(k, 2)
    return base + sum(pieces(b, m) for m in (3, 2, 1) if m > mq) + h


def far_index(b, mq, h):
    return near_index(b, 0, 0) + (pieces(b, 3) if mq else 0) + h


NRECV = near_index(3, 3, 0)


def kernel(a_hbm, out, abuf, part, ring, got, load_sem, a_send, a_recv, z_send, z_recv, t_send, t_recv):
    z = lax.axis_index("kk")
    g = lax.axis_index("g")
    side = z // 2
    inner = ((z + 1) // 2) % 2
    has3 = g % 2
    last = g // 3
    toward = z + 1 - 2 * side
    away = z - 1 + 2 * side

    def mirror(q):
        return q + side * (3 - 2 * q)

    def order(i):
        return mirror(3 - i + inner * (i // 2) * (2 * i - 5))

    def load(k):
        size = (QR, ROWS - QR)[k]
        start = ((1 - side) * (ROWS - QR), side * QR)[k]
        rs = pl.ds(pl.multiple_of(start, QR), size)
        return pltpu.make_async_copy(a_hbm.at[rs], abuf.at[0, rs], load_sem.at[k])

    load(0).start()
    load(1).start()

    bar = pltpu.get_barrier_semaphore()
    for d in (1, NG - 1):
        pl.semaphore_signal(bar, inc=1, device_id={"g": (g + d) % NG}, device_id_type=MESH)
    pl.semaphore_signal(bar, inc=1, device_id={"kk": toward}, device_id_type=MESH)

    @pl.when(inner == 1)
    def _():
        pl.semaphore_signal(bar, inc=1, device_id={"kk": away}, device_id_type=MESH)

    def chunk(q):
        return pl.ds(pl.multiple_of(q * QR, QR), QR)

    def row_copy(src, slot, q, d):
        return pltpu.make_async_remote_copy(
            src.at[chunk(q)], abuf.at[slot, chunk(q)], a_send, a_recv.at[slot - 1, q],
            device_id={"g": (g + d) % NG}, device_id_type=MESH)

    def arrival(slot, q):
        return row_copy(a_hbm, slot, q, NG - 1)

    def dot(x, y):
        return lax.dot_general(x, y, (((1,), (1,)), ((), ())), preferred_element_type=jnp.float32)

    def at(b, q, start, size):
        return pl.ds(pl.multiple_of(b * ROWS + q * QR + start, 16), size)

    def product(b, q):
        left = (0, 1 + last, 2 - last)[b]
        right = (0, last, 0)[b]
        part[at(b, q, 0, QR)] = dot(abuf[left, chunk(q)], abuf[right])

    def part_of(b, d, mq, h):
        if b:
            return h * HALF, HALF, pl.ds(0, ROWS)
        size = SENT[mq]
        start = d * (ROWS - size)
        if mq == 3:
            size = (FIRST, ROWS - FIRST)[h]
            start = ((1 - d) * (ROWS - FIRST), d * FIRST)[h]
        return 0, QR, pl.ds(pl.multiple_of(start, 128), size)

    def z_copy(src, b, d, mq, q, h, dev, index):
        start, size, cs = part_of(b, d, mq, h)
        return pltpu.make_async_remote_copy(
            src.at[at(b, q, start, size), cs], ring.at[d, at(b, q, start, size), cs],
            z_send, z_recv.at[index], device_id={"kk": dev}, device_id_type=MESH)

    def near_copy(src, b, mq, h, index):
        return z_copy(src, b, side, mq, mirror(mq), h, toward, index)

    def far_copy(b, mq, h):
        d = 1 - side
        return z_copy(ring.at[d], b, d, 3 - mq, mirror(mq), h, away, far_index(b, mq, h))

    def wait_near(b, mq, h):
        near_copy(part, b, mq, h, near_index(b, mq, h)).wait_recv()

    def wait_far(b, mq, h):
        far_copy(b, mq, h).wait_recv()

    def send_near(b, mq):
        for h in range(pieces(b, mq)):
            near_copy(part, b, mq, h, near_index(b, mq, h)).start()

    def start():
        q = order(0)
        cs = pl.ds(pl.multiple_of((1 - side) * (ROWS - FIRST), FIRST), FIRST)
        load(0).wait()
        part[at(0, q, 0, QR), cs] = dot(abuf[0, chunk(q)], abuf[0, cs])
        pl.semaphore_wait(bar, 3 + inner)

        @pl.when(inner == 0)
        def _():
            near_copy(part, 0, 3, 0, near_index(0, 3, 0)).start()

        @pl.loop(0, NZ)
        def _(i):
            row_copy(a_hbm, 1, order(i), NG - 1).start()

        @pl.when(g == 2)
        def _():
            @pl.loop(0, NZ)
            def _(i):
                row_copy(a_hbm, 2, order(i), 1).start()

        cs = pl.ds(pl.multiple_of(side * FIRST, FIRST), ROWS - FIRST)
        load(1).wait()
        part[at(0, q, 0, QR), cs] = dot(abuf[0, chunk(q)], abuf[0, cs])

        @pl.when(inner == 0)
        def _():
            near_copy(part, 0, 3, 1, near_index(0, 3, 1)).start()

    def compute(b):
        def step(i):
            q = order(i)
            if b == 1:
                @pl.when(last == 0)
                def _():
                    arrival(1, q).wait_recv()

                @pl.when(g == 2)
                def _():
                    row_copy(abuf.at[1], 2, q, NG - 1).start()

                @pl.when(last == 1)
                def _():
                    arrival(2, q).wait_recv()
            if b == 2:
                @pl.when(g == 1)
                def _():
                    arrival(2, q).wait_recv()
            product(b, q)
            for k in range(0 if b else 1, 3):
                @pl.when((inner == 0) & (i == k))
                def _():
                    send_near(b, 3 - k)

        if b == 1:
            @pl.when(last == 1)
            def _():
                for q in range(NZ):
                    arrival(1, q).wait_recv()
        pl.loop(0 if b else 1, NZ)(step)

    def row_loop(b, q, start, size, body):
        @pl.loop(0, size // 16)
        def _(r):
            body(at(b, q, start + r * 16, 16), pl.ds(pl.multiple_of(start + r * 16, 16), 16))

    def add_in(b, d, mq, q, h):
        start, size, cs = part_of(b, d, mq, h)

        def body(rr, _):
            ring[d, rr, cs] = ring[d, rr, cs] + part[rr, cs]
        row_loop(b, q, start, size, body)

    def group1(b):
        if b == 0:
            turns = ((3, 0), (0, 0), (3, 1), (2, 0), (0, 1))
        else:
            turns = ((3, 0), (3, 1), (0, 0), (2, 0), (0, 1), (2, 1))

        @pl.when(inner == 1)
        def _():
            for mq, h in turns:
                if mq:
                    wait_near(b, mq, h)
                    add_in(b, side, mq, mirror(mq), h)
                    near_copy(ring.at[side], b, mq, h, far_index(b, 3 - mq, h)).start()
                else:
                    wait_far(b, 0, h)
                    add_in(b, 1 - side, 3, mirror(0), h)
                    far_copy(b, 0, h).start()

    def hand_over():
        return pltpu.make_async_remote_copy(
            out.at[2], got, t_send, t_recv, device_id={"g": (g + 1) % NG}, device_id_type=MESH)

    def group2(b):
        slot = (0, 1 + last, (5 - g) // 2)[b]

        @pl.when(inner == 1)
        def _():
            q = mirror(1)
            for h in range(pieces(b, 1)):
                wait_far(b, 1, h)
                wait_near(b, 1, h)
                if b:
                    def body(rr, ro):
                        out[slot, ro] = ring[0, rr] + part[rr] + ring[1, rr]
                    row_loop(b, q, h * HALF, HALF, body)

        if b == 0:
            one, mid = SENT[2], SENT[1]
            lo = ROWS - one

            @pl.when(z == 1)
            def _():
                q1 = pl.ds(QR, QR)
                turned = ring[1, 0:lo, lo:mid].T
                out[0, :, 0:lo] = ring[0, q1, 0:lo] + turned[mid - lo - QR:]
                out[0, :, lo:mid] = ring[0, q1, lo:mid] + part[q1, lo:mid] + ring[1, q1, lo:mid]
                turned = ring[0, 2 * QR:ROWS, lo:mid].T
                out[0, :, mid:] = ring[1, q1, mid:] + turned[mid - lo - QR:]

            @pl.when(z == 2)
            def _():
                q2 = pl.ds(2 * QR, QR)
                turned = ring[0, one:ROWS, mid:one].T
                out[0, :, one:] = ring[1, q2, one:] + turned[:QR]
                out[0, :, mid:one] = ring[0, q2, mid:one] + part[q2, mid:one] + ring[1, q2, mid:one]
                turned = ring[1, 0:2 * QR, mid:one].T
                out[0, :, :mid] = ring[0, q2, :mid] + turned[:QR]

        @pl.when(inner == 0)
        def _():
            q = mirror(0)
            for h in range(pieces(b, 3)):
                wait_far(b, 0, h)
                start, size, cs = part_of(b, 1 - side, 3, h)

                def body(rr, ro):
                    out[slot, ro, cs] = ring[1 - side, rr, cs] + part[rr, cs]
                row_loop(b, q, start, size, body)

        if b == 1:
            @pl.when(last == 1)
            def _():
                hand_over().start()

    def fill(value):
        @pl.loop(0, QR // 16)
        def _(r):
            rs = pl.ds(pl.multiple_of(r * 16, 16), 16)
            out[2, rs] = value(rs)

    start()
    compute(0)
    group1(0)
    compute(1)
    group2(0)
    group1(1)

    @pl.when(has3 == 1)
    def _():
        compute(2)

    group2(1)

    @pl.when(has3 == 1)
    def _():
        group1(2)
        group2(2)

    @pl.when(g == 0)
    def _():
        hand_over().wait_recv()
        fill(lambda rs: got[rs])

    def drain_rows(ref):
        return pltpu.make_async_remote_copy(ref, ref, a_send, a_recv.at[0, 0],
                                            device_id={"g": (g + 1) % NG}, device_id_type=MESH)

    @pl.when(g == 2)
    def _():
        drain_rows(abuf).wait_send()

    @pl.when(g != 2)
    def _():
        drain_rows(abuf.at[0]).wait_send()

    @pl.when(last == 1)
    def _():
        hand_over().wait_send()

    @pl.when(g >= 2)
    def _():
        fill(lambda rs: jnp.zeros((16, ROWS), jnp.float32))

    first = (sum(SENT.values()) * QR // ROWS, (2 * SENT[3] + SENT[2]) * QR // ROWS)
    for i in range(2):
        for k in range(2):
            @pl.when((inner == i) & (has3 == k))
            def _():
                ref = part.at[pl.ds(0, first[i] + (1 + k) * 3 * QR)]
                pltpu.make_async_remote_copy(ref, ref, z_send, z_recv.at[0],
                                             device_id={"kk": toward}, device_id_type=MESH).wait_send()


def solution(mesh):
    def local_fn(a_blk):
        cols = a_blk.shape[1]
        dma = pltpu.SemaphoreType.DMA
        out = pl.pallas_call(
            kernel,
            out_shape=jax.ShapeDtypeStruct((3, QR, ROWS), jnp.float32),
            in_specs=[pl.BlockSpec(memory_space=pltpu.HBM)],
            out_specs=pl.BlockSpec(memory_space=pltpu.VMEM),
            scratch_shapes=[
                pltpu.VMEM((3, ROWS, cols), jnp.bfloat16),
                pltpu.VMEM((3 * ROWS, ROWS), jnp.float32),
                pltpu.VMEM((2, 3 * ROWS, ROWS), jnp.float32),
                pltpu.VMEM((QR, ROWS), jnp.float32),
                dma((2,)), dma, dma((2, NZ)), dma, dma((NRECV,)), dma, dma,
            ],
            compiler_params=pltpu.CompilerParams(
                collective_id=0, has_side_effects=True, vmem_limit_bytes=50 * 2**20),
        )(a_blk)
        return out[None]

    return jax.shard_map(local_fn, mesh=mesh, in_specs=(P(("m", "g"), "kk"),),
                         out_specs=P(("m", "g"), None, "kk", None), check_vma=False)
```

time: 93.5 us -> 92.2 us (0.986)
  Pallas kernels: 92.1 us -> 90.8 us
    pallas_call x1, Pallas kernels: 92.1 us -> 90.8 us  [local_fn(): pl.pallas_call(kernel, out_shape=jax.ShapeDtypeStruct((3, QR, ROWS), jnp....]
where the time goes in v5:
time: 92.2 us; the launch traced here: 92.1 us
  Pallas kernels  90.8 us (98%)
  local copies, waits for them, and re-layouts  1.21 us (1%)
    pallas_call x1, Pallas kernels, local_fn(): pl.pallas_call(kernel, out_shape=jax.ShapeDtypeStruct((3, QR, ROWS), jnp....  90.8 us

profile of v5, /device:TPU:21, one launch (start us, length us, event | category | flops | bytes accessed | tf_op | source)
XLA Modules:
  0.0 92.1 jit_solution(15996327207052262112)
XLA Ops:
  0.0 90.8 %shard_map.17 = f32[3,192,768]{2,1,0:T(8,128)S(1)} custom-call(bf16[768,2048]{1,0:T(8,128)(2,1)} %a_hbm.1), custom_call_target="tpu_custom_call" | custom-call | tf_op jit(solution)/shard_map/pallas_call | solution.py:335
  90.9 1.2 %copy.3 = f32[1,3,192,768]{3,2,1,0:T(8,128)} copy(f32[1,3,192,768]{3,2,1,0:T(8,128)S(1)} %bitcast.1) | data formatting | bytes 3538944

commit v6 on v5

--- a/solution.py
+++ b/solution.py
@@ -12,11 +12,17 @@
 QR = ROWS // NZ
 HALF = QR // 2
 FIRST = 128
-SENT = {3: 768, 2: 640, 1: 384}
+ONE, MID = 640, 384
+SENT = {
+    3: ((0, QR, ONE, FIRST), (64, QR - 64, 0, ONE), (0, 64, 0, MID), (0, 64, 512, FIRST)),
+    2: ((0, QR, 0, ONE),),
+    1: ((0, QR, 0, MID),),
+}
+EXTRA = (0, 64, MID, FIRST)
 
 
 def pieces(b, mq):
-    return (1 if mq < 3 else 2) if b == 0 else 2
+    return 2 if b else len(SENT[mq])
 
 
 def near_index(b, mq, h):
@@ -30,7 +36,12 @@
     return near_index(b, 0, 0) + (pieces(b, 3) if mq else 0) + h
 
 
-NRECV = near_index(3, 3, 0)
+NEXTRA = near_index(3, 3, 0)
+NRECV = NEXTRA + 1
+
+
+def elements(parts):
+    return sum(p[1] * p[3] for p in parts)
 
 
 def kernel(a_hbm, out, abuf, part, ring, got, load_sem, a_send, a_recv, z_send, z_recv, t_send, t_recv):
@@ -89,28 +100,33 @@
         right = (0, last, 0)[b]
         part[at(b, q, 0, QR)] = dot(abuf[left, chunk(q)], abuf[right])
 
-    def part_of(b, d, mq, h):
+    def part_of(b, d, piece):
         if b:
-            return h * HALF, HALF, pl.ds(0, ROWS)
-        size = SENT[mq]
-        start = d * (ROWS - size)
-        if mq == 3:
-            size = (FIRST, ROWS - FIRST)[h]
-            start = ((1 - d) * (ROWS - FIRST), d * FIRST)[h]
-        return 0, QR, pl.ds(pl.multiple_of(start, 128), size)
-
-    def z_copy(src, b, d, mq, q, h, dev, index):
-        start, size, cs = part_of(b, d, mq, h)
+            return piece * HALF, HALF, pl.ds(0, ROWS)
+        row, nrows, col, ncols = piece
+        row = row + d * (QR - 2 * row - nrows)
+        col = col + d * (ROWS - 2 * col - ncols)
+        return row, nrows, pl.ds(pl.multiple_of(col, 128), ncols)
+
+    def piece_of(b, mq, h):
+        return h if b else SENT[mq][h]
+
+    def z_copy(src, b, d, piece, q, dev, index):
+        start, size, cs = part_of(b, d, piece)
         return pltpu.make_async_remote_copy(
             src.at[at(b, q, start, size), cs], ring.at[d, at(b, q, start, size), cs],
             z_send, z_recv.at[index], device_id={"kk": dev}, device_id_type=MESH)
 
     def near_copy(src, b, mq, h, index):
-        return z_copy(src, b, side, mq, mirror(mq), h, toward, index)
+        return z_copy(src, b, side, piece_of(b, mq, h), mirror(mq), toward, index)
 
     def far_copy(b, mq, h):
         d = 1 - side
-        return z_copy(ring.at[d], b, d, 3 - mq, mirror(mq), h, away, far_index(b, mq, h))
+        return z_copy(ring.at[d], b, d, piece_of(b, 3 - mq, h), mirror(mq), away, far_index(b, mq, h))
+
+    def extra_copy():
+        d = 1 - side
+        return z_copy(ring.at[d], 0, d, EXTRA, mirror(0), away, NEXTRA)
 
     def wait_near(b, mq, h):
         near_copy(part, b, mq, h, near_index(b, mq, h)).wait_recv()
@@ -149,7 +165,8 @@
 
         @pl.when(inner == 0)
         def _():
-            near_copy(part, 0, 3, 1, near_index(0, 3, 1)).start()
+            for h in range(1, pieces(0, 3)):
+                near_copy(part, 0, 3, h, near_index(0, 3, h)).start()
 
     def compute(b):
         def step(i):
@@ -189,7 +206,7 @@
             body(at(b, q, start + r * 16, 16), pl.ds(pl.multiple_of(start + r * 16, 16), 16))
 
     def add_in(b, d, mq, q, h):
-        start, size, cs = part_of(b, d, mq, h)
+        start, size, cs = part_of(b, d, piece_of(b, mq, h))
 
         def body(rr, _):
             ring[d, rr, cs] = ring[d, rr, cs] + part[rr, cs]
@@ -197,7 +214,7 @@
 
     def group1(b):
         if b == 0:
-            turns = ((3, 0), (0, 0), (3, 1), (2, 0), (0, 1))
+            turns = ((3, 0), (0, 0), (3, 1), (3, 2), (3, 3), (2, 0), (0, 1), (0, 2), (0, 3))
         else:
             turns = ((3, 0), (3, 1), (0, 0), (2, 0), (0, 1), (2, 1))
 
@@ -217,6 +234,17 @@
         return pltpu.make_async_remote_copy(
             out.at[2], got, t_send, t_recv, device_id={"g": (g + 1) % NG}, device_id_type=MESH)
 
+    def fill_in():
+        @pl.when(z == 1)
+        def _():
+            turned = ring[1, 256:384, 128:256].T
+            ring[1, 128:192, 256:384] = turned[:64] + part[128:192, 256:384]
+
+        @pl.when(z == 2)
+        def _():
+            turned = ring[0, 384:512, 512:640].T
+            ring[0, 576:640, 384:512] = turned[64:] + part[576:640, 384:512]
+
     def group2(b):
         slot = (0, 1 + last, (5 - g) // 2)[b]
 
@@ -225,6 +253,9 @@
             q = mirror(1)
             for h in range(pieces(b, 1)):
                 wait_far(b, 1, h)
+                if b == 0:
+                    fill_in()
+                    extra_copy().start()
                 wait_near(b, 1, h)
                 if b:
                     def body(rr, ro):
@@ -232,37 +263,43 @@
                     row_loop(b, q, h * HALF, HALF, body)
 
         if b == 0:
-            one, mid = SENT[2], SENT[1]
-            lo = ROWS - one
+            lo = ROWS - ONE
 
             @pl.when(z == 1)
             def _():
                 q1 = pl.ds(QR, QR)
-                turned = ring[1, 0:lo, lo:mid].T
-                out[0, :, 0:lo] = ring[0, q1, 0:lo] + turned[mid - lo - QR:]
-                out[0, :, lo:mid] = ring[0, q1, lo:mid] + part[q1, lo:mid] + ring[1, q1, lo:mid]
-                turned = ring[0, 2 * QR:ROWS, lo:mid].T
-                out[0, :, mid:] = ring[1, q1, mid:] + turned[mid - lo - QR:]
+                turned = ring[1, 0:lo, lo:MID].T
+                out[0, :, 0:lo] = ring[0, q1, 0:lo] + turned[MID - lo - QR:]
+                out[0, :, lo:MID] = ring[0, q1, lo:MID] + part[q1, lo:MID] + ring[1, q1, lo:MID]
+                turned = ring[0, 2 * QR:ROWS, lo:MID].T
+                out[0, :, MID:] = ring[1, q1, MID:] + turned[MID - lo - QR:]
 
             @pl.when(z == 2)
             def _():
                 q2 = pl.ds(2 * QR, QR)
-                turned = ring[0, one:ROWS, mid:one].T
-                out[0, :, one:] = ring[1, q2, one:] + turned[:QR]
-                out[0, :, mid:one] = ring[0, q2, mid:one] + part[q2, mid:one] + ring[1, q2, mid:one]
-                turned = ring[1, 0:2 * QR, mid:one].T
-                out[0, :, :mid] = ring[0, q2, :mid] + turned[:QR]
+                turned = ring[0, ONE:ROWS, MID:ONE].T
+                out[0, :, ONE:] = ring[1, q2, ONE:] + turned[:QR]
+                out[0, :, MID:ONE] = ring[0, q2, MID:ONE] + part[q2, MID:ONE] + ring[1, q2, MID:ONE]
+                turned = ring[1, 0:2 * QR, MID:ONE].T
+                out[0, :, :MID] = ring[0, q2, :MID] + turned[:QR]
 
         @pl.when(inner == 0)
         def _():
             q = mirror(0)
-            for h in range(pieces(b, 3)):
-                wait_far(b, 0, h)
-                start, size, cs = part_of(b, 1 - side, 3, h)
+
+            def add_out(piece):
+                start, size, cs = part_of(b, 1 - side, piece)
 
                 def body(rr, ro):
                     out[slot, ro, cs] = ring[1 - side, rr, cs] + part[rr, cs]
                 row_loop(b, q, start, size, body)
+
+            for h in range(pieces(b, 3)):
+                wait_far(b, 0, h)
+                add_out(piece_of(b, 3, h))
+            if b == 0:
+                extra_copy().wait_recv()
+                add_out(EXTRA)
 
         if b == 1:
             @pl.when(last == 1)
@@ -318,12 +355,13 @@
     def _():
         fill(lambda rs: jnp.zeros((16, ROWS), jnp.float32))
 
-    first = (sum(SENT.values()) * QR // ROWS, (2 * SENT[3] + SENT[2]) * QR // ROWS)
+    first = (elements(SENT[3] + SENT[2] + SENT[1]), elements(2 * SENT[3] + SENT[2] + (EXTRA,)))
     for i in range(2):
         for k in range(2):
             @pl.when((inner == i) & (has3 == k))
             def _():
-                ref = part.at[pl.ds(0, first[i] + (1 + k) * 3 * QR)]
+                total = first[i] + (1 + k) * 3 * QR * ROWS
+                ref = ring.at[:, pl.ds(0, total // 1024), pl.ds(0, 512)]
                 pltpu.make_async_remote_copy(ref, ref, z_send, z_recv.at[0],
                                              device_id={"kk": toward}, device_id_type=MESH).wait_send()
 

time: 92.2 us -> 91.6 us (level)
  no operation moved by 1% of the time
where the time goes in v6:
time: 91.6 us; the launch traced here: 91.4 us
  Pallas kernels  90.2 us (98%)
  local copies, waits for them, and re-layouts  1.21 us (1%)
    pallas_call x1, Pallas kernels, local_fn(): pl.pallas_call(kernel, out_shape=jax.ShapeDtypeStruct((3, QR, ROWS), jnp....  90.2 us

profile of v6, /device:TPU:21, one launch (start us, length us, event | category | flops | bytes accessed | tf_op | source)
XLA Modules:
  0.0 91.4 jit_solution(7390812781705411916)
XLA Ops:
  0.0 90.2 %shard_map.17 = f32[3,192,768]{2,1,0:T(8,128)S(1)} custom-call(bf16[768,2048]{1,0:T(8,128)(2,1)} %a_hbm.1), custom_call_target="tpu_custom_call" | custom-call | tf_op jit(solution)/shard_map/pallas_call | solution.py:373
  90.2 1.2 %copy.3 = f32[1,3,192,768]{3,2,1,0:T(8,128)} copy(f32[1,3,192,768]{3,2,1,0:T(8,128)S(1)} %bitcast.1) | data formatting | bytes 3538944

commit v7 on v6

--- a/solution.py
+++ b/solution.py
@@ -12,13 +12,12 @@
 QR = ROWS // NZ
 HALF = QR // 2
 FIRST = 128
-ONE, MID = 640, 384
+TILE = 128
 SENT = {
-    3: ((0, QR, ONE, FIRST), (64, QR - 64, 0, ONE), (0, 64, 0, MID), (0, 64, 512, FIRST)),
-    2: ((0, QR, 0, ONE),),
-    1: ((0, QR, 0, MID),),
+    3: ((64, TILE, ROWS - FIRST, FIRST), (0, QR, 0, ROWS - FIRST)),
+    2: ((0, QR, 0, 512), (128, 64, 512, TILE)),
+    1: ((0, QR, 0, 256), (64, 128, 256, TILE)),
 }
-EXTRA = (0, 64, MID, FIRST)
 
 
 def pieces(b, mq):
@@ -36,8 +35,7 @@
     return near_index(b, 0, 0) + (pieces(b, 3) if mq else 0) + h
 
 
-NEXTRA = near_index(3, 3, 0)
-NRECV = NEXTRA + 1
+NRECV = near_index(3, 3, 0)
 
 
 def elements(parts):
@@ -124,10 +122,6 @@
         d = 1 - side
         return z_copy(ring.at[d], b, d, piece_of(b, 3 - mq, h), mirror(mq), away, far_index(b, mq, h))
 
-    def extra_copy():
-        d = 1 - side
-        return z_copy(ring.at[d], 0, d, EXTRA, mirror(0), away, NEXTRA)
-
     def wait_near(b, mq, h):
         near_copy(part, b, mq, h, near_index(b, mq, h)).wait_recv()
 
@@ -168,17 +162,13 @@
             for h in range(1, pieces(0, 3)):
                 near_copy(part, 0, 3, h, near_index(0, 3, h)).start()
 
-    def compute(b):
+    def compute(b, first, stop):
         def step(i):
             q = order(i)
             if b == 1:
-                @pl.when(last == 0)
+                @pl.when(g < 2)
                 def _():
                     arrival(1, q).wait_recv()
-
-                @pl.when(g == 2)
-                def _():
-                    row_copy(abuf.at[1], 2, q, NG - 1).start()
 
                 @pl.when(last == 1)
                 def _():
@@ -188,17 +178,17 @@
                 def _():
                     arrival(2, q).wait_recv()
             product(b, q)
-            for k in range(0 if b else 1, 3):
+            for k in range(first, min(stop, 3)):
                 @pl.when((inner == 0) & (i == k))
                 def _():
                     send_near(b, 3 - k)
 
-        if b == 1:
+        if b == 1 and first == 0:
             @pl.when(last == 1)
             def _():
                 for q in range(NZ):
                     arrival(1, q).wait_recv()
-        pl.loop(0 if b else 1, NZ)(step)
+        pl.loop(first, stop)(step)
 
     def row_loop(b, q, start, size, body):
         @pl.loop(0, size // 16)
@@ -214,7 +204,7 @@
 
     def group1(b):
         if b == 0:
-            turns = ((3, 0), (0, 0), (3, 1), (3, 2), (3, 3), (2, 0), (0, 1), (0, 2), (0, 3))
+            turns = ((3, 0), (0, 0), (3, 1), (2, 0), (2, 1), (0, 1))
         else:
             turns = ((3, 0), (3, 1), (0, 0), (2, 0), (0, 1), (2, 1))
 
@@ -234,16 +224,39 @@
         return pltpu.make_async_remote_copy(
             out.at[2], got, t_send, t_recv, device_id={"g": (g + 1) % NG}, device_id_type=MESH)
 
-    def fill_in():
-        @pl.when(z == 1)
-        def _():
-            turned = ring[1, 256:384, 128:256].T
-            ring[1, 128:192, 256:384] = turned[:64] + part[128:192, 256:384]
-
-        @pl.when(z == 2)
-        def _():
-            turned = ring[0, 384:512, 512:640].T
-            ring[0, 576:640, 384:512] = turned[64:] + part[576:640, 384:512]
+    def finish_inner(q, near, far, turn):
+        low = turn == 0
+
+        def cols(start, size):
+            return pl.ds(start if low else ROWS - start - size, size)
+
+        def rows_of(start, size):
+            return cols(start, size)
+
+        def turned(d, row, nrows, narrow):
+            x = ring[d, rows_of(row, nrows), cols(128 if narrow else 256, TILE)].T
+            if narrow:
+                x = x[64:] if low else x[:64]
+            return x
+
+        def put(row, nrows, col, ncols, value):
+            start = (row if low else ROWS - row - nrows) - q * QR
+            out[0, start:start + nrows, cols(col, ncols)] = value
+
+        def get(ref, row, nrows, col, ncols):
+            return ref[rows_of(row, nrows), cols(col, ncols)]
+
+        n, f = ring.at[near], ring.at[far]
+        a, b = (192, 64), (256, 128)
+        put(*a, 0, 128, get(n, *a, 0, 128) + turned(far, 0, 128, True))
+        put(*a, 128, 128, get(n, *a, 128, 128) + get(part, *a, 128, 128) + get(f, *a, 128, 128))
+        put(*a, 256, 128, turned(near, 256, 128, True) + get(part, *a, 256, 128) + get(f, *a, 256, 128))
+        put(*a, 384, 384, turned(near, 384, 384, True) + get(f, *a, 384, 384))
+        lane = lax.broadcasted_iota(jnp.int32, (128, 256), 1)
+        mine = jnp.where(lane >= 192 if low else lane < 64, get(part, *b, 0, 256), 0.0)
+        put(*b, 0, 256, get(n, *b, 0, 256) + turned(far, 0, 256, False) + mine)
+        put(*b, 256, 128, get(n, *b, 256, 128) + get(part, *b, 256, 128) + get(f, *b, 256, 128))
+        put(*b, 384, 384, turned(near, 384, 384, False) + get(f, *b, 384, 384))
 
     def group2(b):
         slot = (0, 1 + last, (5 - g) // 2)[b]
@@ -253,9 +266,6 @@
             q = mirror(1)
             for h in range(pieces(b, 1)):
                 wait_far(b, 1, h)
-                if b == 0:
-                    fill_in()
-                    extra_copy().start()
                 wait_near(b, 1, h)
                 if b:
                     def body(rr, ro):
@@ -263,25 +273,13 @@
                     row_loop(b, q, h * HALF, HALF, body)
 
         if b == 0:
-            lo = ROWS - ONE
-
             @pl.when(z == 1)
             def _():
-                q1 = pl.ds(QR, QR)
-                turned = ring[1, 0:lo, lo:MID].T
-                out[0, :, 0:lo] = ring[0, q1, 0:lo] + turned[MID - lo - QR:]
-                out[0, :, lo:MID] = ring[0, q1, lo:MID] + part[q1, lo:MID] + ring[1, q1, lo:MID]
-                turned = ring[0, 2 * QR:ROWS, lo:MID].T
-                out[0, :, MID:] = ring[1, q1, MID:] + turned[MID - lo - QR:]
+                finish_inner(1, 0, 1, 0)
 
             @pl.when(z == 2)
             def _():
-                q2 = pl.ds(2 * QR, QR)
-                turned = ring[0, ONE:ROWS, MID:ONE].T
-                out[0, :, ONE:] = ring[1, q2, ONE:] + turned[:QR]
-                out[0, :, MID:ONE] = ring[0, q2, MID:ONE] + part[q2, MID:ONE] + ring[1, q2, MID:ONE]
-                turned = ring[1, 0:2 * QR, MID:ONE].T
-                out[0, :, :MID] = ring[0, q2, :MID] + turned[:QR]
+                finish_inner(2, 1, 0, 1)
 
         @pl.when(inner == 0)
         def _():
@@ -297,9 +295,17 @@
             for h in range(pieces(b, 3)):
                 wait_far(b, 0, h)
                 add_out(piece_of(b, 3, h))
-            if b == 0:
-                extra_copy().wait_recv()
-                add_out(EXTRA)
+
+        if b == 0:
+            @pl.when(z == 0)
+            def _():
+                turned = ring[1, 0:128, 128:256].T
+                out[0, 128:192, 0:128] = part[128:192, 0:128] + turned[:64]
+
+            @pl.when(z == 3)
+            def _():
+                turned = ring[0, 640:768, 512:640].T
+                out[0, 0:64, 640:768] = part[576:640, 640:768] + turned[64:]
 
         if b == 1:
             @pl.when(last == 1)
@@ -313,21 +319,32 @@
             out[2, rs] = value(rs)
 
     start()
-    compute(0)
+    compute(0, 1, NZ)
+
+    @pl.when(g == 2)
+    def _():
+        @pl.loop(0, NZ)
+        def _(i):
+            q = order(i)
+            arrival(1, q).wait_recv()
+            row_copy(abuf.at[1], 2, q, NG - 1).start()
+
     group1(0)
-    compute(1)
+    compute(1, 0, 3)
     group2(0)
     group1(1)
+    compute(1, 3, NZ)
 
     @pl.when(has3 == 1)
     def _():
-        compute(2)
+        compute(2, 0, 3)
 
     group2(1)
 
     @pl.when(has3 == 1)
     def _():
         group1(2)
+        compute(2, 3, NZ)
         group2(2)
 
     @pl.when(g == 0)
@@ -355,7 +372,7 @@
     def _():
         fill(lambda rs: jnp.zeros((16, ROWS), jnp.float32))
 
-    first = (elements(SENT[3] + SENT[2] + SENT[1]), elements(2 * SENT[3] + SENT[2] + (EXTRA,)))
+    first = (elements(SENT[3] + SENT[2] + SENT[1]), elements(2 * SENT[3] + SENT[2]))
     for i in range(2):
         for k in range(2):
             @pl.when((inner == i) & (has3 == k))

time: 91.6 us -> 89.6 us (0.978)
  Pallas kernels: 90.2 us -> 88.2 us
    pallas_call x1, Pallas kernels: 90.2 us -> 88.2 us  [local_fn(): pl.pallas_call(kernel, out_shape=jax.ShapeDtypeStruct((3, QR, ROWS), jnp....]
where the time goes in v7:
time: 89.6 us; the launch traced here: 89.4 us
  Pallas kernels  88.2 us (98%)
  local copies, waits for them, and re-layouts  1.21 us (1%)
    pallas_call x1, Pallas kernels, local_fn(): pl.pallas_call(kernel, out_shape=jax.ShapeDtypeStruct((3, QR, ROWS), jnp....  88.2 us

profile of v7, /device:TPU:21, one launch (start us, length us, event | category | flops | bytes accessed | tf_op | source)
XLA Modules:
  0.0 89.4 jit_solution(3000556977328118944)
XLA Ops:
  0.0 88.2 %shard_map.17 = f32[3,192,768]{2,1,0:T(8,128)S(1)} custom-call(bf16[768,2048]{1,0:T(8,128)(2,1)} %a_hbm.1), custom_call_target="tpu_custom_call" | custom-call | tf_op jit(solution)/shard_map/pallas_call | solution.py:390
  88.2 1.2 %copy.3 = f32[1,3,192,768]{3,2,1,0:T(8,128)} copy(f32[1,3,192,768]{3,2,1,0:T(8,128)S(1)} %bitcast.1) | data formatting | bytes 3538944

commit v8 on v7

--- a/solution.py
+++ b/solution.py
@@ -11,13 +11,14 @@
 ROWS = 768
 QR = ROWS // NZ
 HALF = QR // 2
-FIRST = 128
+FIRST = 256
 TILE = 128
 SENT = {
-    3: ((64, TILE, ROWS - FIRST, FIRST), (0, QR, 0, ROWS - FIRST)),
-    2: ((0, QR, 0, 512), (128, 64, 512, TILE)),
-    1: ((0, QR, 0, 256), (64, 128, 256, TILE)),
+    3: ((0, QR, 512, TILE), (128, 64, 640, TILE), (0, QR, 0, 512)),
+    2: ((0, QR, 0, 384), (64, 128, 384, TILE)),
+    1: ((0, QR, 0, 256), (128, 64, 256, TILE)),
 }
+PACKED = ((384, 512), (256, 640))
 
 
 def pieces(b, mq):
@@ -42,7 +43,8 @@
     return sum(p[1] * p[3] for p in parts)
 
 
-def kernel(a_hbm, out, abuf, part, ring, got, load_sem, a_send, a_recv, z_send, z_recv, t_send, t_recv):
+def kernel(a_hbm, out, abuf, part, ring, got, pack_in, pack_out, load_sem, a_send, a_recv, z_send, z_recv,
+           p_recv, t_send, t_recv):
     z = lax.axis_index("kk")
     g = lax.axis_index("g")
     side = z // 2
@@ -59,9 +61,9 @@
         return mirror(3 - i + inner * (i // 2) * (2 * i - 5))
 
     def load(k):
-        size = (QR, ROWS - QR)[k]
-        start = ((1 - side) * (ROWS - QR), side * QR)[k]
-        rs = pl.ds(pl.multiple_of(start, QR), size)
+        size = (FIRST, ROWS - FIRST)[k]
+        start = ((1 - side) * (ROWS - FIRST), side * FIRST)[k]
+        rs = pl.ds(pl.multiple_of(start, FIRST), size)
         return pltpu.make_async_copy(a_hbm.at[rs], abuf.at[0, rs], load_sem.at[k])
 
     load(0).start()
@@ -141,7 +143,8 @@
 
         @pl.when(inner == 0)
         def _():
-            near_copy(part, 0, 3, 0, near_index(0, 3, 0)).start()
+            for h in range(2):
+                near_copy(part, 0, 3, h, near_index(0, 3, h)).start()
 
         @pl.loop(0, NZ)
         def _(i):
@@ -159,8 +162,7 @@
 
         @pl.when(inner == 0)
         def _():
-            for h in range(1, pieces(0, 3)):
-                near_copy(part, 0, 3, h, near_index(0, 3, h)).start()
+            near_copy(part, 0, 3, 2, near_index(0, 3, 2)).start()
 
     def compute(b, first, stop):
         def step(i):
@@ -204,7 +206,7 @@
 
     def group1(b):
         if b == 0:
-            turns = ((3, 0), (0, 0), (3, 1), (2, 0), (2, 1), (0, 1))
+            turns = ((3, 0), (3, 1), (0, 0), (0, 1), (3, 2), (2, 0), (2, 1), (0, 2))
         else:
             turns = ((3, 0), (3, 1), (0, 0), (2, 0), (0, 1), (2, 1))
 
@@ -224,42 +226,101 @@
         return pltpu.make_async_remote_copy(
             out.at[2], got, t_send, t_recv, device_id={"g": (g + 1) % NG}, device_id_type=MESH)
 
-    def finish_inner(q, near, far, turn):
-        low = turn == 0
-
-        def cols(start, size):
-            return pl.ds(start if low else ROWS - start - size, size)
-
-        def rows_of(start, size):
-            return cols(start, size)
-
-        def turned(d, row, nrows, narrow):
-            x = ring[d, rows_of(row, nrows), cols(128 if narrow else 256, TILE)].T
-            if narrow:
-                x = x[64:] if low else x[:64]
-            return x
+    def flip(d, start, size):
+        return pl.ds(ROWS - start - size if d else start, size)
+
+    def get(ref, d, row, nrows, col, ncols):
+        return ref[flip(d, row, nrows), flip(d, col, ncols)]
+
+    def keep(d, x, y):
+        lane = lax.broadcasted_iota(jnp.int32, x.shape, 1)
+        return jnp.where(lane >= 64 if d else lane < 64, x, y)
+
+    def roll(x):
+        return pltpu.roll(x, 64, 1)
+
+    def pack(d, slot):
+        x, y = (get(part, d, row, 64, row, TILE) for row in PACKED[slot])
+        return keep(d, x, roll(y))
+
+    def unpack(d, slot, second):
+        x = pack_in[d, pl.ds(slot * 64, 64)]
+        return roll(x) if second else x
+
+    def pack_copy(d, dev):
+        return pltpu.make_async_remote_copy(
+            pack_out.at[d], pack_in.at[d], z_send, p_recv.at[d], device_id={"kk": dev}, device_id_type=MESH)
+
+    def pack_end(d):
+        for slot in range(2):
+            pack_out[d, pl.ds(slot * 64, 64)] = pack(d, slot)
+        pack_copy(d, toward).start()
+
+    def pack_pass(d, dev):
+        pack_copy(d, dev).wait_recv()
+        for slot in range(2):
+            rs = pl.ds(slot * 64, 64)
+            pack_out[d, rs] = pack_in[d, rs] + pack(d, slot)
+        pack_copy(d, dev).start()
+
+    def halves(d, x):
+        return (x[64:], x[:64]) if d else (x[:64], x[64:])
+
+    def finish_inner(q, near, far):
+        d = near
 
         def put(row, nrows, col, ncols, value):
-            start = (row if low else ROWS - row - nrows) - q * QR
-            out[0, start:start + nrows, cols(col, ncols)] = value
-
-        def get(ref, row, nrows, col, ncols):
-            return ref[rows_of(row, nrows), cols(col, ncols)]
+            start = (ROWS - row - nrows if d else row) - q * QR
+            out[0, start:start + nrows, flip(d, col, ncols)] = value
+
+        def turned(ref, row, nrows, col):
+            return get(ref, d, row, nrows, col, TILE).T
+
+        def narrow(ref, row, nrows):
+            return halves(d, turned(ref, row, nrows, 128))[1]
 
         n, f = ring.at[near], ring.at[far]
         a, b = (192, 64), (256, 128)
-        put(*a, 0, 128, get(n, *a, 0, 128) + turned(far, 0, 128, True))
-        put(*a, 128, 128, get(n, *a, 128, 128) + get(part, *a, 128, 128) + get(f, *a, 128, 128))
-        put(*a, 256, 128, turned(near, 256, 128, True) + get(part, *a, 256, 128) + get(f, *a, 256, 128))
-        put(*a, 384, 384, turned(near, 384, 384, True) + get(f, *a, 384, 384))
+        put(*a, 0, 128, get(n, d, *a, 0, 128) + narrow(f, 0, 128))
+        x = keep(d, narrow(f, 128, 128), unpack(far, 0, True) + get(part, d, *a, 128, 128))
+        put(*a, 128, 128, get(n, d, *a, 128, 128) + x)
+        put(*a, 256, 128, narrow(n, 256, 128) + get(part, d, *a, 256, 128) + get(f, d, *a, 256, 128))
+        put(*a, 384, 384, narrow(n, 384, 384) + get(f, d, *a, 384, 384))
         lane = lax.broadcasted_iota(jnp.int32, (128, 256), 1)
-        mine = jnp.where(lane >= 192 if low else lane < 64, get(part, *b, 0, 256), 0.0)
-        put(*b, 0, 256, get(n, *b, 0, 256) + turned(far, 0, 256, False) + mine)
-        put(*b, 256, 128, get(n, *b, 256, 128) + get(part, *b, 256, 128) + get(f, *b, 256, 128))
-        put(*b, 384, 384, turned(near, 384, 384, False) + get(f, *b, 384, 384))
+        mine = jnp.where(lane < 64 if d else lane >= 192, get(part, d, *b, 0, 256), 0.0)
+        put(*b, 0, 256, get(n, d, *b, 0, 256) + turned(f, 0, 256, 256) + mine)
+        top, low = (256, 64, 256, 128), (320, 64, 256, 128)
+        x = keep(d, unpack(near, 1, False), halves(d, turned(n, *b, 256))[0])
+        put(*top, x + get(part, d, *top) + get(f, d, *top))
+        x = keep(d, halves(d, turned(f, *b, 256))[1], unpack(far, 0, False))
+        put(*low, get(n, d, *low) + get(part, d, *low) + x)
+        put(*b, 384, 384, turned(n, 384, 384, 256) + get(f, d, *b, 384, 384))
+
+    def finish_end(far):
+        d = 1 - far
+        q = 0 if d == 0 else NZ - 1
+
+        def put(row, nrows, col, ncols, value):
+            start = (ROWS - row - nrows if d else row) - q * QR
+            out[0, start:start + nrows, flip(d, col, ncols)] = value + get(part, d, row, nrows, col, ncols)
+
+        f = ring.at[far]
+        x = halves(d, get(f, d, 0, 128, 0, TILE).T)[1]
+        put(64, 64, 0, TILE, keep(d, x, unpack(far, 1, True)))
+        put(128, 64, 0, TILE, halves(d, get(f, d, 0, 128, 128, TILE).T)[0])
 
     def group2(b):
         slot = (0, 1 + last, (5 - g) // 2)[b]
+        if b == 0:
+            @pl.when(z == 1)
+            def _():
+                pack_pass(0, toward)
+                pack_pass(1, away)
+
+            @pl.when(z == 2)
+            def _():
+                pack_pass(1, toward)
+                pack_pass(0, away)
 
         @pl.when(inner == 1)
         def _():
@@ -275,11 +336,11 @@
         if b == 0:
             @pl.when(z == 1)
             def _():
-                finish_inner(1, 0, 1, 0)
+                finish_inner(1, 0, 1)
 
             @pl.when(z == 2)
             def _():
-                finish_inner(2, 1, 0, 1)
+                finish_inner(2, 1, 0)
 
         @pl.when(inner == 0)
         def _():
@@ -299,13 +360,13 @@
         if b == 0:
             @pl.when(z == 0)
             def _():
-                turned = ring[1, 0:128, 128:256].T
-                out[0, 128:192, 0:128] = part[128:192, 0:128] + turned[:64]
+                pack_copy(1, toward).wait_recv()
+                finish_end(1)
 
             @pl.when(z == 3)
             def _():
-                turned = ring[0, 640:768, 512:640].T
-                out[0, 0:64, 640:768] = part[576:640, 640:768] + turned[64:]
+                pack_copy(0, toward).wait_recv()
+                finish_end(0)
 
         if b == 1:
             @pl.when(last == 1)
@@ -321,6 +382,14 @@
     start()
     compute(0, 1, NZ)
 
+    @pl.when(z == 0)
+    def _():
+        pack_end(0)
+
+    @pl.when(z == 3)
+    def _():
+        pack_end(1)
+
     @pl.when(g == 2)
     def _():
         @pl.loop(0, NZ)
@@ -372,7 +441,8 @@
     def _():
         fill(lambda rs: jnp.zeros((16, ROWS), jnp.float32))
 
-    first = (elements(SENT[3] + SENT[2] + SENT[1]), elements(2 * SENT[3] + SENT[2]))
+    packed = TILE * TILE
+    first = (elements(SENT[3] + SENT[2] + SENT[1]) + packed, elements(2 * SENT[3] + SENT[2]) + 2 * packed)
     for i in range(2):
         for k in range(2):
             @pl.when((inner == i) & (has3 == k))
@@ -397,7 +467,9 @@
                 pltpu.VMEM((3 * ROWS, ROWS), jnp.float32),
                 pltpu.VMEM((2, 3 * ROWS, ROWS), jnp.float32),
                 pltpu.VMEM((QR, ROWS), jnp.float32),
-                dma((2,)), dma, dma((2, NZ)), dma, dma((NRECV,)), dma, dma,
+                pltpu.VMEM((2, TILE, TILE), jnp.float32),
+                pltpu.VMEM((2, TILE, TILE), jnp.float32),
+                dma((2,)), dma, dma((2, NZ)), dma, dma((NRECV,)), dma((2,)), dma, dma,
             ],
             compiler_params=pltpu.CompilerParams(
                 collective_id=0, has_side_effects=True, vmem_limit_bytes=50 * 2**20),

time: 89.6 us -> 88.1 us (0.983)
  Pallas kernels: 88.2 us -> 86.8 us
    pallas_call x1, Pallas kernels: 88.2 us -> 86.8 us  [local_fn(): pl.pallas_call(kernel, out_shape=jax.ShapeDtypeStruct((3, QR, ROWS), jnp....]
where the time goes in v8:
time: 88.1 us; the launch traced here: 88 us
  Pallas kernels  86.8 us (99%)
  local copies, waits for them, and re-layouts  1.21 us (1%)
    pallas_call x1, Pallas kernels, local_fn(): pl.pallas_call(kernel, out_shape=jax.ShapeDtypeStruct((3, QR, ROWS), jnp....  86.8 us

profile of v8, /device:TPU:21, one launch (start us, length us, event | category | flops | bytes accessed | tf_op | source)
XLA Modules:
  0.0 88.0 jit_solution(14170480216724194846)
XLA Ops:
  0.0 86.8 %shard_map.17 = f32[3,192,768]{2,1,0:T(8,128)S(1)} custom-call(bf16[768,2048]{1,0:T(8,128)(2,1)} %a_hbm.1), custom_call_target="tpu_custom_call" | custom-call | tf_op jit(solution)/shard_map/pallas_call | solution.py:460
  86.8 1.2 %copy.3 = f32[1,3,192,768]{3,2,1,0:T(8,128)} copy(f32[1,3,192,768]{3,2,1,0:T(8,128)S(1)} %bitcast.1) | data formatting | bytes 3538944

commit v9 on v8

--- a/solution.py
+++ b/solution.py
@@ -14,11 +14,12 @@
 FIRST = 256
 TILE = 128
 SENT = {
-    3: ((0, QR, 512, TILE), (128, 64, 640, TILE), (0, QR, 0, 512)),
-    2: ((0, QR, 0, 384), (64, 128, 384, TILE)),
-    1: ((0, QR, 0, 256), (128, 64, 256, TILE)),
+    3: ((64, 128, 512, TILE), (0, QR, 0, 512)),
+    2: ((0, QR, 0, 384), (128, 64, 384, TILE)),
+    1: ((0, QR, 0, 256),),
 }
-PACKED = ((384, 512), (256, 640))
+TILES = (256, 384, 512, 640)
+PACK = 64 * len(TILES) + 8
 
 
 def pieces(b, mq):
@@ -44,7 +45,7 @@
 
 
 def kernel(a_hbm, out, abuf, part, ring, got, pack_in, pack_out, load_sem, a_send, a_recv, z_send, z_recv,
-           p_recv, t_send, t_recv):
+           p_send, p_recv, t_send, t_recv):
     z = lax.axis_index("kk")
     g = lax.axis_index("g")
     side = z // 2
@@ -143,8 +144,7 @@
 
         @pl.when(inner == 0)
         def _():
-            for h in range(2):
-                near_copy(part, 0, 3, h, near_index(0, 3, h)).start()
+            near_copy(part, 0, 3, 0, near_index(0, 3, 0)).start()
 
         @pl.loop(0, NZ)
         def _(i):
@@ -162,7 +162,7 @@
 
         @pl.when(inner == 0)
         def _():
-            near_copy(part, 0, 3, 2, near_index(0, 3, 2)).start()
+            near_copy(part, 0, 3, 1, near_index(0, 3, 1)).start()
 
     def compute(b, first, stop):
         def step(i):
@@ -206,7 +206,7 @@
 
     def group1(b):
         if b == 0:
-            turns = ((3, 0), (3, 1), (0, 0), (0, 1), (3, 2), (2, 0), (2, 1), (0, 2))
+            turns = ((3, 0), (0, 0), (3, 1), (2, 0), (2, 1), (0, 1))
         else:
             turns = ((3, 0), (3, 1), (0, 0), (2, 0), (0, 1), (2, 1))
 
@@ -232,39 +232,53 @@
     def get(ref, d, row, nrows, col, ncols):
         return ref[flip(d, row, nrows), flip(d, col, ncols)]
 
-    def keep(d, x, y):
-        lane = lax.broadcasted_iota(jnp.int32, x.shape, 1)
-        return jnp.where(lane >= 64 if d else lane < 64, x, y)
-
     def roll(x):
         return pltpu.roll(x, 64, 1)
 
-    def pack(d, slot):
-        x, y = (get(part, d, row, 64, row, TILE) for row in PACKED[slot])
-        return keep(d, x, roll(y))
-
-    def unpack(d, slot, second):
-        x = pack_in[d, pl.ds(slot * 64, 64)]
-        return roll(x) if second else x
+    def masks(d):
+        row = lax.broadcasted_iota(jnp.int32, (64, TILE), 0)
+        lane = lax.broadcasted_iota(jnp.int32, (64, TILE), 1)
+        if d:
+            return (lane >= 64) | (row > lane), row == lane
+        return (lane < 64) | (row < lane - 64), row == lane - 64
+
+    def halves(d, x):
+        return (x[64:], x[:64]) if d else (x[:64], x[64:])
+
+    def pack(d):
+        plain, diagonal = masks(d)
+        body, rows = [], []
+        for row in TILES:
+            first, second = halves(d, get(part, d, row, TILE, row, TILE))
+            body.append(jnp.where(plain, second, roll(first)))
+            rows.append(jnp.sum(jnp.where(diagonal, second, 0.0), axis=0, keepdims=True))
+        return jnp.concatenate(body + rows + [jnp.zeros((4, TILE), jnp.float32)], axis=0)
+
+    def unpack(d, k):
+        plain, diagonal = masks(d)
+        row = lax.broadcasted_iota(jnp.int32, (64, TILE), 0)
+        lane = lax.broadcasted_iota(jnp.int32, (64, TILE), 1)
+        x = pack_in[d, k * 64:k * 64 + 64]
+        y = roll(x)
+        turned = jnp.concatenate([x, y] if d else [y, x], axis=0).T
+        first, second = halves(d, turned)
+        second = jnp.where(plain, x, jnp.where(diagonal, pack_in[d, PACK - 8 + k:PACK - 7 + k], second))
+        own = (lane >= 64) & (row <= lane - 64) if d else (lane < 64) & (row >= lane)
+        first = jnp.where(own, y, first)
+        return jnp.concatenate([second, first] if d else [first, second], axis=0)
 
     def pack_copy(d, dev):
         return pltpu.make_async_remote_copy(
-            pack_out.at[d], pack_in.at[d], z_send, p_recv.at[d], device_id={"kk": dev}, device_id_type=MESH)
+            pack_out.at[d], pack_in.at[d], p_send.at[d], p_recv.at[d], device_id={"kk": dev}, device_id_type=MESH)
 
     def pack_end(d):
-        for slot in range(2):
-            pack_out[d, pl.ds(slot * 64, 64)] = pack(d, slot)
+        pack_out[d] = pack(d)
         pack_copy(d, toward).start()
 
     def pack_pass(d, dev):
         pack_copy(d, dev).wait_recv()
-        for slot in range(2):
-            rs = pl.ds(slot * 64, 64)
-            pack_out[d, rs] = pack_in[d, rs] + pack(d, slot)
+        pack_out[d] = pack_in[d] + pack(d)
         pack_copy(d, dev).start()
-
-    def halves(d, x):
-        return (x[64:], x[:64]) if d else (x[:64], x[64:])
 
     def finish_inner(q, near, far):
         d = near
@@ -282,18 +296,14 @@
         n, f = ring.at[near], ring.at[far]
         a, b = (192, 64), (256, 128)
         put(*a, 0, 128, get(n, d, *a, 0, 128) + narrow(f, 0, 128))
-        x = keep(d, narrow(f, 128, 128), unpack(far, 0, True) + get(part, d, *a, 128, 128))
-        put(*a, 128, 128, get(n, d, *a, 128, 128) + x)
+        x = halves(d, unpack(far, 2))[1]
+        put(*a, 128, 128, get(n, d, *a, 128, 128) + get(part, d, *a, 128, 128) + x)
         put(*a, 256, 128, narrow(n, 256, 128) + get(part, d, *a, 256, 128) + get(f, d, *a, 256, 128))
         put(*a, 384, 384, narrow(n, 384, 384) + get(f, d, *a, 384, 384))
         lane = lax.broadcasted_iota(jnp.int32, (128, 256), 1)
         mine = jnp.where(lane < 64 if d else lane >= 192, get(part, d, *b, 0, 256), 0.0)
         put(*b, 0, 256, get(n, d, *b, 0, 256) + turned(f, 0, 256, 256) + mine)
-        top, low = (256, 64, 256, 128), (320, 64, 256, 128)
-        x = keep(d, unpack(near, 1, False), halves(d, turned(n, *b, 256))[0])
-        put(*top, x + get(part, d, *top) + get(f, d, *top))
-        x = keep(d, halves(d, turned(f, *b, 256))[1], unpack(far, 0, False))
-        put(*low, get(n, d, *low) + get(part, d, *low) + x)
+        put(*b, 256, 128, unpack(near, 0) + get(part, d, *b, 256, 128) + unpack(far, 1))
         put(*b, 384, 384, turned(n, 384, 384, 256) + get(f, d, *b, 384, 384))
 
     def finish_end(far):
@@ -305,9 +315,9 @@
             out[0, start:start + nrows, flip(d, col, ncols)] = value + get(part, d, row, nrows, col, ncols)
 
         f = ring.at[far]
-        x = halves(d, get(f, d, 0, 128, 0, TILE).T)[1]
-        put(64, 64, 0, TILE, keep(d, x, unpack(far, 1, True)))
+        put(0, 128, 0, TILE, unpack(far, 3))
         put(128, 64, 0, TILE, halves(d, get(f, d, 0, 128, 128, TILE).T)[0])
+        put(128, 64, 128, TILE, halves(d, unpack(far, 2))[0])
 
     def group2(b):
         slot = (0, 1 + last, (5 - g) // 2)[b]
@@ -325,9 +335,11 @@
         @pl.when(inner == 1)
         def _():
             q = mirror(1)
-            for h in range(pieces(b, 1)):
-                wait_far(b, 1, h)
-                wait_near(b, 1, h)
+            for h in range(2):
+                if h < pieces(b, 2):
+                    wait_far(b, 1, h)
+                if h < pieces(b, 1):
+                    wait_near(b, 1, h)
                 if b:
                     def body(rr, ro):
                         out[slot, ro] = ring[0, rr] + part[rr] + ring[1, rr]
@@ -441,8 +453,13 @@
     def _():
         fill(lambda rs: jnp.zeros((16, ROWS), jnp.float32))
 
-    packed = TILE * TILE
-    first = (elements(SENT[3] + SENT[2] + SENT[1]) + packed, elements(2 * SENT[3] + SENT[2]) + 2 * packed)
+    pack_copy(side, toward).wait_send()
+
+    @pl.when(inner == 1)
+    def _():
+        pack_copy(1 - side, toward).wait_send()
+
+    first = (elements(SENT[3] + SENT[2] + SENT[1]), elements(2 * SENT[3] + SENT[2]))
     for i in range(2):
         for k in range(2):
             @pl.when((inner == i) & (has3 == k))
@@ -467,9 +484,9 @@
                 pltpu.VMEM((3 * ROWS, ROWS), jnp.float32),
                 pltpu.VMEM((2, 3 * ROWS, ROWS), jnp.float32),
                 pltpu.VMEM((QR, ROWS), jnp.float32),
-                pltpu.VMEM((2, TILE, TILE), jnp.float32),
-                pltpu.VMEM((2, TILE, TILE), jnp.float32),
-                dma((2,)), dma, dma((2, NZ)), dma, dma((NRECV,)), dma((2,)), dma, dma,
+                pltpu.VMEM((2, PACK, TILE), jnp.float32),
+                pltpu.VMEM((2, PACK, TILE), jnp.float32),
+                dma((2,)), dma, dma((2, NZ)), dma, dma((NRECV,)), dma((2,)), dma((2,)), dma, dma,
             ],
             compiler_params=pltpu.CompilerParams(
                 collective_id=0, has_side_effects=True, vmem_limit_bytes=50 * 2**20),

time: 88.1 us -> 86.9 us (0.986)
  Pallas kernels: 86.8 us -> 85.6 us
    pallas_call x1, Pallas kernels: 86.8 us -> 85.6 us  [local_fn(): pl.pallas_call(kernel, out_shape=jax.ShapeDtypeStruct((3, QR, ROWS), jnp....]
where the time goes in v9:
time: 86.9 us; the launch traced here: 86.8 us
  Pallas kernels  85.6 us (99%)
  local copies, waits for them, and re-layouts  1.21 us (1%)
    pallas_call x1, Pallas kernels, local_fn(): pl.pallas_call(kernel, out_shape=jax.ShapeDtypeStruct((3, QR, ROWS), jnp....  85.6 us

profile of v9, /device:TPU:21, one launch (start us, length us, event | category | flops | bytes accessed | tf_op | source)
XLA Modules:
  0.0 86.8 jit_solution(2894187198127890018)
XLA Ops:
  0.0 85.6 %shard_map.17 = f32[3,192,768]{2,1,0:T(8,128)S(1)} custom-call(bf16[768,2048]{1,0:T(8,128)(2,1)} %a_hbm.1), custom_call_target="tpu_custom_call" | custom-call | tf_op jit(solution)/shard_map/pallas_call | solution.py:477
  85.6 1.2 %copy.3 = f32[1,3,192,768]{3,2,1,0:T(8,128)} copy(f32[1,3,192,768]{3,2,1,0:T(8,128)S(1)} %bitcast.1) | data formatting | bytes 3538944

commit v10 on v9

--- a/solution.py
+++ b/solution.py
@@ -23,7 +23,7 @@
 
 
 def pieces(b, mq):
-    return 2 if b else len(SENT[mq])
+    return (len(SENT[mq]), 1, 2)[b]
 
 
 def near_index(b, mq, h):
@@ -103,7 +103,8 @@
 
     def part_of(b, d, piece):
         if b:
-            return piece * HALF, HALF, pl.ds(0, ROWS)
+            size = QR // pieces(b, 3)
+            return piece * size, size, pl.ds(0, ROWS)
         row, nrows, col, ncols = piece
         row = row + d * (QR - 2 * row - nrows)
         col = col + d * (ROWS - 2 * col - ncols)
@@ -205,10 +206,9 @@
         row_loop(b, q, start, size, body)
 
     def group1(b):
-        if b == 0:
-            turns = ((3, 0), (0, 0), (3, 1), (2, 0), (2, 1), (0, 1))
-        else:
-            turns = ((3, 0), (3, 1), (0, 0), (2, 0), (0, 1), (2, 1))
+        turns = (((3, 0), (0, 0), (3, 1), (2, 0), (2, 1), (0, 1)),
+                 ((3, 0), (2, 0), (0, 0)),
+                 ((3, 0), (3, 1), (0, 0), (2, 0), (0, 1), (2, 1)))[b]
 
         @pl.when(inner == 1)
         def _():
@@ -340,10 +340,10 @@
                     wait_far(b, 1, h)
                 if h < pieces(b, 1):
                     wait_near(b, 1, h)
-                if b:
+                if b and h < pieces(b, 1):
                     def body(rr, ro):
                         out[slot, ro] = ring[0, rr] + part[rr] + ring[1, rr]
-                    row_loop(b, q, h * HALF, HALF, body)
+                    row_loop(b, q, *part_of(b, 0, h)[:2], body)
 
         if b == 0:
             @pl.when(z == 1)
@@ -426,12 +426,6 @@
     def _():
         group1(2)
         compute(2, 3, NZ)
-        group2(2)
-
-    @pl.when(g == 0)
-    def _():
-        hand_over().wait_recv()
-        fill(lambda rs: got[rs])
 
     def drain_rows(ref):
         return pltpu.make_async_remote_copy(ref, ref, a_send, a_recv.at[0, 0],
@@ -458,6 +452,15 @@
     @pl.when(inner == 1)
     def _():
         pack_copy(1 - side, toward).wait_send()
+
+    @pl.when(has3 == 1)
+    def _():
+        group2(2)
+
+    @pl.when(g == 0)
+    def _():
+        hand_over().wait_recv()
+        fill(lambda rs: got[rs])
 
     first = (elements(SENT[3] + SENT[2] + SENT[1]), elements(2 * SENT[3] + SENT[2]))
     for i in range(2):

time: 86.9 us -> 86.8 us (level)
  no operation moved by 1% of the time
where the time goes in v10:
time: 86.8 us; the launch traced here: 86.7 us
  Pallas kernels  85.4 us (98%)
  local copies, waits for them, and re-layouts  1.21 us (1%)
    pallas_call x1, Pallas kernels, local_fn(): pl.pallas_call(kernel, out_shape=jax.ShapeDtypeStruct((3, QR, ROWS), jnp....  85.4 us

profile of v10, /device:TPU:21, one launch (start us, length us, event | category | flops | bytes accessed | tf_op | source)
XLA Modules:
  0.0 86.7 jit_solution(11078448026540451423)
XLA Ops:
  0.0 85.4 %shard_map.17 = f32[3,192,768]{2,1,0:T(8,128)S(1)} custom-call(bf16[768,2048]{1,0:T(8,128)(2,1)} %a_hbm.1), custom_call_target="tpu_custom_call" | custom-call | tf_op jit(solution)/shard_map/pallas_call | solution.py:480
  85.5 1.2 %copy.3 = f32[1,3,192,768]{3,2,1,0:T(8,128)} copy(f32[1,3,192,768]{3,2,1,0:T(8,128)S(1)} %bitcast.1) | data formatting | bytes 3538944

commit v11 on v10

--- a/solution.py
+++ b/solution.py
@@ -27,17 +27,19 @@
 
 
 def near_index(b, mq, h):
-    base = 0
-    for k in range(b):
-        base += sum(pieces(k, m) for m in (3, 2, 1)) + pieces(k, 3) + pieces(k, 2)
+    if b == 0:
+        return 0 if mq == 3 else 1
+    base = 4 if b == 1 else 4 + sum(pieces(1, m) for m in (3, 2, 1, 3, 2))
     return base + sum(pieces(b, m) for m in (3, 2, 1) if m > mq) + h
 
 
 def far_index(b, mq, h):
+    if b == 0:
+        return 2 + mq
     return near_index(b, 0, 0) + (pieces(b, 3) if mq else 0) + h
 
 
-NRECV = near_index(3, 3, 0)
+NRECV = far_index(2, 1, pieces(2, 2))
 
 
 def elements(parts):
@@ -126,11 +128,22 @@
         d = 1 - side
         return z_copy(ring.at[d], b, d, piece_of(b, 3 - mq, h), mirror(mq), away, far_index(b, mq, h))
 
+    def wait_all(index, parts):
+        ref = ring.at[:, pl.ds(0, elements(parts) // 1024), pl.ds(0, 512)]
+        pltpu.make_async_remote_copy(ref, ref, z_send, z_recv.at[index], device_id={"kk": toward},
+                                     device_id_type=MESH).wait_recv()
+
     def wait_near(b, mq, h):
-        near_copy(part, b, mq, h, near_index(b, mq, h)).wait_recv()
+        if b:
+            near_copy(part, b, mq, h, near_index(b, mq, h)).wait_recv()
+        elif h == 0 and mq > 1:
+            wait_all(near_index(0, mq, 0), SENT[3] if mq == 3 else SENT[2] + SENT[1])
 
     def wait_far(b, mq, h):
-        far_copy(b, mq, h).wait_recv()
+        if b:
+            far_copy(b, mq, h).wait_recv()
+        elif h == 0:
+            wait_all(far_index(0, mq, 0), SENT[3 - mq])
 
     def send_near(b, mq):
         for h in range(pieces(b, mq)):
@@ -206,7 +219,7 @@
         row_loop(b, q, start, size, body)
 
     def group1(b):
-        turns = (((3, 0), (0, 0), (3, 1), (2, 0), (2, 1), (0, 1)),
+        turns = (((3, 0), (3, 1), (2, 0), (2, 1), (0, 0), (0, 1)),
                  ((3, 0), (2, 0), (0, 0)),
                  ((3, 0), (3, 1), (0, 0), (2, 0), (0, 1), (2, 1)))[b]
 
@@ -269,7 +282,7 @@
 
     def pack_copy(d, dev):
         return pltpu.make_async_remote_copy(
-            pack_out.at[d], pack_in.at[d], p_send.at[d], p_recv.at[d], device_id={"kk": dev}, device_id_type=MESH)
+            pack_out.at[d], pack_in.at[d], p_send, p_recv.at[d], device_id={"kk": dev}, device_id_type=MESH)
 
     def pack_end(d):
         pack_out[d] = pack(d)
@@ -447,11 +460,14 @@
     def _():
         fill(lambda rs: jnp.zeros((16, ROWS), jnp.float32))
 
-    pack_copy(side, toward).wait_send()
+    @pl.when(inner == 0)
+    def _():
+        pack_copy(side, toward).wait_send()
 
     @pl.when(inner == 1)
     def _():
-        pack_copy(1 - side, toward).wait_send()
+        pltpu.make_async_remote_copy(pack_out, pack_in, p_send, p_recv.at[0], device_id={"kk": toward},
+                                     device_id_type=MESH).wait_send()
 
     @pl.when(has3 == 1)
     def _():
@@ -489,7 +505,7 @@
                 pltpu.VMEM((QR, ROWS), jnp.float32),
                 pltpu.VMEM((2, PACK, TILE), jnp.float32),
                 pltpu.VMEM((2, PACK, TILE), jnp.float32),
-                dma((2,)), dma, dma((2, NZ)), dma, dma((NRECV,)), dma((2,)), dma((2,)), dma, dma,
+                dma((2,)), dma, dma((2, NZ)), dma, dma((NRECV,)), dma, dma((2,)), dma, dma,
             ],
             compiler_params=pltpu.CompilerParams(
                 collective_id=0, has_side_effects=True, vmem_limit_bytes=50 * 2**20),

time: 86.8 us -> 86.8 us (level)
  no operation moved by 1% of the time
where the time goes in v11:
time: 86.8 us; the launch traced here: 86.6 us
  Pallas kernels  85.4 us (98%)
  local copies, waits for them, and re-layouts  1.21 us (1%)
    pallas_call x1, Pallas kernels, local_fn(): pl.pallas_call(kernel, out_shape=jax.ShapeDtypeStruct((3, QR, ROWS), jnp....  85.4 us

profile of v11, /device:TPU:21, one launch (start us, length us, event | category | flops | bytes accessed | tf_op | source)
XLA Modules:
  0.0 86.6 jit_solution(7722608619093643511)
XLA Ops:
  0.0 85.4 %shard_map.17 = f32[3,192,768]{2,1,0:T(8,128)S(1)} custom-call(bf16[768,2048]{1,0:T(8,128)(2,1)} %a_hbm.1), custom_call_target="tpu_custom_call" | custom-call | tf_op jit(solution)/shard_map/pallas_call | solution.py:496
  85.4 1.2 %copy.3 = f32[1,3,192,768]{3,2,1,0:T(8,128)} copy(f32[1,3,192,768]{3,2,1,0:T(8,128)S(1)} %bitcast.1) | data formatting | bytes 3538944

commit v12 on v11

--- a/solution.py
+++ b/solution.py
@@ -207,9 +207,9 @@
         pl.loop(first, stop)(step)
 
     def row_loop(b, q, start, size, body):
-        @pl.loop(0, size // 16)
+        @pl.loop(0, size // 32)
         def _(r):
-            body(at(b, q, start + r * 16, 16), pl.ds(pl.multiple_of(start + r * 16, 16), 16))
+            body(at(b, q, start + r * 32, 32), pl.ds(pl.multiple_of(start + r * 32, 32), 32))
 
     def add_in(b, d, mq, q, h):
         start, size, cs = part_of(b, d, piece_of(b, mq, h))

time: 86.8 us -> 86.7 us (level)
  no operation moved by 1% of the time
where the time goes in v12:
time: 86.7 us; the launch traced here: 86.6 us
  Pallas kernels  85.4 us (99%)
  local copies, waits for them, and re-layouts  1.21 us (1%)
    pallas_call x1, Pallas kernels, local_fn(): pl.pallas_call(kernel, out_shape=jax.ShapeDtypeStruct((3, QR, ROWS), jnp....  85.4 us

profile of v12, /device:TPU:21, one launch (start us, length us, event | category | flops | bytes accessed | tf_op | source)
XLA Modules:
  0.0 86.6 jit_solution(13264607713345374779)
XLA Ops:
  0.0 85.4 %shard_map.17 = f32[3,192,768]{2,1,0:T(8,128)S(1)} custom-call(bf16[768,2048]{1,0:T(8,128)(2,1)} %a_hbm.1), custom_call_target="tpu_custom_call" | custom-call | tf_op jit(solution)/shard_map/pallas_call | solution.py:496
  85.4 1.2 %copy.3 = f32[1,3,192,768]{3,2,1,0:T(8,128)} copy(f32[1,3,192,768]{3,2,1,0:T(8,128)S(1)} %bitcast.1) | data formatting | bytes 3538944

commit v13 on v12

--- a/solution.py
+++ b/solution.py
@@ -207,7 +207,7 @@
         pl.loop(first, stop)(step)
 
     def row_loop(b, q, start, size, body):
-        @pl.loop(0, size // 32)
+        @pl.loop(0, size // 32, unroll=True)
         def _(r):
             body(at(b, q, start + r * 32, 32), pl.ds(pl.multiple_of(start + r * 32, 32), 32))
 

time: 86.7 us -> 86.7 us (level)
  no operation moved by 1% of the time
where the time goes in v13:
time: 86.7 us; the launch traced here: 86.6 us
  Pallas kernels  85.4 us (99%)
  local copies, waits for them, and re-layouts  1.21 us (1%)
    pallas_call x1, Pallas kernels, local_fn(): pl.pallas_call(kernel, out_shape=jax.ShapeDtypeStruct((3, QR, ROWS), jnp....  85.4 us

profile of v13, /device:TPU:21, one launch (start us, length us, event | category | flops | bytes accessed | tf_op | source)
XLA Modules:
  0.0 86.6 jit_solution(1807366154541648000)
XLA Ops:
  0.0 85.4 %shard_map.17 = f32[3,192,768]{2,1,0:T(8,128)S(1)} custom-call(bf16[768,2048]{1,0:T(8,128)(2,1)} %a_hbm.1), custom_call_target="tpu_custom_call" | custom-call | tf_op jit(solution)/shard_map/pallas_call | solution.py:496
  85.4 1.2 %copy.3 = f32[1,3,192,768]{3,2,1,0:T(8,128)} copy(f32[1,3,192,768]{3,2,1,0:T(8,128)S(1)} %bitcast.1) | data formatting | bytes 3538944
